TPU v7x, 8 devices: a whole 2x2x1 slice. The times are simulated.
8 devices in a mesh: rep: 1 (over z), tp: 2 (over y), ep: 4 (over x, core).
Axes of the slice: x: 2, y: 2, z: 1, core: 2. Of those that a mesh axis runs over, the one named last changes fastest.
Arguments:
- x_in: bfloat16 [8192, 2048], P(('rep', 'ep'))
- route_ids: int32 [2, 8192, 2], P(None, ('rep', 'ep'))
- gate_vals: float32 [2, 8192, 2], P(None, ('rep', 'ep'))
- w_gate: bfloat16 [2, 4, 2048, 5504], P(None, ('rep', 'ep'), None, 'tp')
- w_up: bfloat16 [2, 4, 2048, 5504], P(None, ('rep', 'ep'), None, 'tp')
- w_down: bfloat16 [2, 4, 5504, 2048], P(None, ('rep', 'ep'), 'tp')
- old_map: int32 [2, 4], replicated
- move_src: int32 [2, 2], replicated
- move_dst: int32 [2, 2], replicated
Outputs:
- output 1: bfloat16 [8192, 2048], P(('rep', 'ep'))
- output 2: bfloat16 [2, 4, 2048, 5504], P(None, ('rep', 'ep'), None, 'tp')
- output 3: bfloat16 [2, 4, 2048, 5504], P(None, ('rep', 'ep'), None, 'tp')
- output 4: bfloat16 [2, 4, 5504, 2048], P(None, ('rep', 'ep'), 'tp')
All inputs are finite; a program needn't handle non-finite values.
Results may differ from a plain program's by a relative error of at most 0.00772671.
Values are sent between devices in bfloat16 or wider.
A program may use at most 1 GiB of HBM per device.

v0:
```python
import jax
import jax.numpy as jnp
from jax import lax
from jax.sharding import PartitionSpec as P


def slot_table(slot_map, all_slots):
    return jax.ops.segment_min(jnp.arange(all_slots, dtype=jnp.int32), slot_map, num_segments=all_slots)


def moe_layer(hidden, layer_ids, layer_gates, w_gate, w_up, w_down, first_slot, group_size, capacity):
    tokens, top_k = layer_ids.shape
    local_slots = w_gate.shape[0]
    model_dim = hidden.shape[1]
    all_slots = group_size * local_slots
    slot_flat = first_slot[layer_ids.reshape(-1)]
    one_hot = (slot_flat[:, None] == jnp.arange(all_slots, dtype=jnp.int32)[None, :]).astype(jnp.int32)
    slot_rank = jnp.sum(jnp.cumsum(one_hot, axis=0) * one_hot, axis=1) - 1
    dest_row = slot_flat * capacity + slot_rank
    row_token = jnp.full((all_slots * capacity,), tokens, jnp.int32).at[dest_row].set(jnp.arange(tokens * top_k, dtype=jnp.int32) // top_k)
    padded = jnp.concatenate([hidden, jnp.zeros((1, model_dim), hidden.dtype)], axis=0)
    send_rows = padded[row_token].reshape(group_size, local_slots, capacity, model_dim)
    recv_rows = lax.all_to_all(send_rows, 'ep', 0, 2, tiled=True).reshape(local_slots, group_size * capacity, model_dim)
    gate_acc = jnp.einsum('scd,sdf->scf', recv_rows, w_gate, preferred_element_type=jnp.float32)
    up_acc = jnp.einsum('scd,sdf->scf', recv_rows, w_up, preferred_element_type=jnp.float32)
    hidden_act = (jax.nn.silu(gate_acc) * up_acc).astype(jnp.bfloat16)
    part_out = jnp.einsum('scf,sfd->scd', hidden_act, w_down, preferred_element_type=jnp.float32)
    expert_out = lax.psum(part_out, 'tp').astype(jnp.bfloat16)
    returned = lax.all_to_all(expert_out.reshape(1, local_slots, group_size * capacity, model_dim), 'ep', 2, 0, tiled=True)
    back_rows = returned.reshape(all_slots * capacity, model_dim)[dest_row].reshape(tokens, top_k, model_dim)
    mixture = jnp.sum(layer_gates[:, :, None] * back_rows, axis=1)
    return (hidden.astype(jnp.float32) + mixture).astype(jnp.bfloat16)


def outgoing_rows(weights, move_src, my_rank, local_slots):
    owns_src = ((move_src // local_slots) == my_rank)[:, None, None]
    src_local = move_src % local_slots
    return tuple(jnp.where(owns_src, w_arr[src_local], jnp.zeros((), w_arr.dtype)) for w_arr in weights)


def install(weights, incoming, move_dst, my_rank, local_slots):
    my_slots = my_rank * local_slots + jnp.arange(local_slots, dtype=jnp.int32)
    dst_match = my_slots[:, None] == move_dst[None, :]
    has_move = jnp.any(dst_match, axis=1)[:, None, None]
    move_pick = jnp.argmax(dst_match, axis=1)
    return tuple(jnp.where(has_move, inc_arr[move_pick], w_arr) for inc_arr, w_arr in zip(incoming, weights))


def solution(mesh):
    group_size = mesh.shape['ep']
    row_spec = P(('rep', 'ep'), None)
    layer_spec = P(None, ('rep', 'ep'), None)
    col_spec = P(None, ('rep', 'ep'), None, 'tp')
    down_spec = P(None, ('rep', 'ep'), 'tp', None)
    map_spec = P(None, None)

    def device_step(x_in, route_ids, gate_vals, w_gate, w_up, w_down, old_map, move_src, move_dst):
        local_slots = w_gate.shape[1]
        tokens, top_k = route_ids.shape[1], route_ids.shape[2]
        all_slots = group_size * local_slots
        capacity = 2 * tokens * top_k // all_slots
        my_rank = lax.axis_index('ep')
        hidden = x_in
        new_sets = []
        for layer_idx in range(2):
            weights = (w_gate[layer_idx], w_up[layer_idx], w_down[layer_idx])
            incoming = lax.psum(outgoing_rows(weights, move_src[layer_idx], my_rank, local_slots), 'ep')
            weights = install(weights, incoming, move_dst[layer_idx], my_rank, local_slots)
            new_map = old_map[layer_idx].at[move_dst[layer_idx]].set(old_map[layer_idx][move_src[layer_idx]])
            first_slot = slot_table(new_map, all_slots)
            hidden = moe_layer(hidden, route_ids[layer_idx], gate_vals[layer_idx], weights[0], weights[1], weights[2], first_slot, group_size, capacity)
            new_sets.append(weights)
        return (hidden, jnp.stack([new_sets[0][0], new_sets[1][0]]), jnp.stack([new_sets[0][1], new_sets[1][1]]), jnp.stack([new_sets[0][2], new_sets[1][2]]))

    return jax.shard_map(device_step, mesh=mesh, in_specs=(row_spec, layer_spec, layer_spec, col_spec, col_spec, down_spec, map_spec, map_spec, map_spec), out_specs=(row_spec, col_spec, col_spec, down_spec), check_vma=False)
```

profile of v0, /device:TPU:0, one launch (start us, length us, event | category | flops | bytes accessed | tf_op | source)
XLA Modules:
  0.0 9030.3 jit_solution(15081221717855620201)
XLA Ops:
  7.2 17.2 slice_bitcast_fusion.2
  38.2 13.2 slice_bitcast_fusion
  60.4 21.2 broadcast_select_fusion.4
  81.6 21.5 broadcast_select_fusion.1
  123.1 15.5 scatter_custom_fusion.2
  138.7 65.9 gather_fusion.1
  204.6 10.3 all-to-all-start
  218.0 720.5 %all-to-all-done = bf16[4,1,2048,2048]{3,2,1,0:T(8,128)(2,1)} async-done(((bf16[4,1,2048,2048]{3,2,1,0:T(8,128)(2,1)}), bf16[4,1,2048,2048]{3,2,1,0:T(8,128)(2,1)}, u32[]{:S(2)}, u32[]{:S(2)}) %all-to-all-start) | async-done | bytes 33554464 | tf_op jit(solution)/shard_map/all_to_all | solution.py:23
  938.5 1354.3 %all-reduce.10.cloned.1.call-done = (bf16[2,2048,2752]{1,2,0:T(8,128)(2,1)}, bf16[2,2048,2752]{1,2,0:T(8,128)(2,1)}, bf16[2,2752,2048]{2,1,0:T(8,128)(2,1)}, bf1...) async-done(((bf16[2,2048,2752]{1,2,0:T(8,128)(2,1)}, bf16[2,2048,2752]{1,2,0:T(8,128)(2,1)}, bf16[2,2752,2048]{2,1,0:T(8,128)(2,1)}, bf16[2,2048,2752]{1,2,0:T(8,128)(2,1)}, ...) | async-done | bytes 112721936 | tf_op jit(solution)/shard_map/psum | solution.py:67
  2292.8 105.7 %fusion.4 = f32[8192,2752]{0,1:T(8,128)} fusion(bf16[8192,2048]{1,0:T(8,128)(2,1)} %bitcast.17, pred[]{:T(512)} %get-tuple-element.75, bf16[2,2048,2752]{1,2,0:T(8,128)(2,1)} %get-tuple-element.76, s32[]{:T(128)} %bitcast.20, bf16[2,1,2048,2752]{2,3,1,0:T(8,128)(2,1)} %param.12), kind=kOutput, calls=%fused_computation.48 | convolution fusion | flops 92347432960 | bytes 146277376 | tf_op jit(solution)/shard_map/scd,sdf->scf/dot_general | solution.py:24
  2398.5 261.0 %multiply_convert_fusion.1 = bf16[8192,2752]{0,1:T(8,128)(2,1)} fusion(f32[8192,2752]{0,1:T(8,128)} %fusion.4, bf16[8192,2048]{1,0:T(8,128)(2,1)} %bitcast.17, pred[]{:T(512)} %get-tuple-element.75, bf16[2,2048,2752]{1,2,0:T(8,128)(2,1)} %get-tuple-element.77, s32[]{:T(128)} %bitcast.20, bf16[2,1,2048,2752]{2,3,1,0:T(8,128)(2,1)} %param.13), kind=kOutput, calls=%fused_computation.13 | convolution fusion | flops 92482699264 | bytes 191366144 | tf_op jit(solution)/shard_map/scd,sdf->scf/dot_general | solution.py:25
  2659.5 110.2 %convolution_bitcast_fusion.1 = f32[1,8192,2048]{2,1,0:T(8,128)} fusion(bf16[8192,2752]{0,1:T(8,128)(2,1)} %multiply_convert_fusion.1, pred[]{:T(512)} %get-tuple-element.75, bf16[2,2752,2048]{2,1,0:T(8,128)(2,1)} %get-tuple-element.78, s32[]{:T(128)} %bitcast.20, bf16[2,1,2752,2048]{3,2,1,0:T(8,128)(2,1)} %param.14), kind=kOutput, calls=%fused_computation.15 | convolution fusion | flops 92347432960 | bytes 134743040 | tf_op jit(solution)/shard_map/scf,sfd->scd/dot_general | solution.py:27
  2769.7 1513.1 %all-reduce.11 = bf16[1,8192,2048]{2,1,0:T(8,128)(2,1)} all-reduce(f32[1,8192,2048]{2,1,0:T(8,128)} %convolution_bitcast_fusion.1), channel_id=1, replica_groups=mesh['rep'=1,'tp'=2,'ep'=4] {'tp'}, use_global_device_ids=true, to_apply=%region_11.12 | all-reduce | flops 16777216 | bytes 100663296 | tf_op jit(solution)/shard_map/psum | solution.py:28
  4282.8 56.6 copy.48
  4340.0 196.0 %reduce.37 = bf16[8192,2048]{1,0:T(8,128)(2,1)} reduce(bf16[8192,1,1,2048]{3,2,1,0:T(2,128)(2,1)} %bitcast.211, bf16[]{:T(256)} %broadcast.635), dimensions={1,2}, to_apply=%bitcast.211.reduce_sub_computation | reduce | bytes 67108864
  4535.9 50.4 reshape.869
  4605.2 15.7 scatter_custom_fusion.5
  4621.0 337.6 %all-to-all-done.1 = bf16[4,2,2097152]{2,1,0:T(2,128)(2,1)} async-done(((bf16[4,2,2097152]{2,1,0:T(2,128)(2,1)}), bf16[4,2,2097152]{2,1,0:T(2,128)(2,1)}, u32[]{:S(2)}, u32[]{:S(2)}) %all-to-all-start.1) | async-done | bytes 33554464 | tf_op jit(solution)/shard_map/all_to_all | solution.py:29
  4958.6 74.2 reshape.870
  5032.8 41.1 copy.46
  5073.9 95.4 %gather_fusion.2 = bf16[4096,2048]{1,0:T(8,128)(2,1)} fusion(bf16[8192,2048]{1,0:T(8,128)(2,1)} %bitcast.214, s32[4096]{0:T(1024)S(1)} %broadcast_clamp_fusion.1), kind=kCustom, calls=%fused_computation.2 | custom fusion | bytes 33570816 | tf_op jit(solution)/shard_map/gather | solution.py:30
  5169.3 35.0 reshape.701
  5204.4 57.0 multiply_reduce_fusion.1
  5261.4 12.0 add_convert_fusion.1
  5281.8 65.8 gather_fusion.4
  5347.6 9.9 all-to-all-start.2
  5357.6 13.9 broadcast_select_fusion
  5374.3 680.8 %all-to-all-done.2 = bf16[4,1,2048,2048]{3,2,1,0:T(8,128)(2,1)} async-done(((bf16[4,1,2048,2048]{3,2,1,0:T(8,128)(2,1)}), bf16[4,1,2048,2048]{3,2,1,0:T(8,128)(2,1)}, u32[]{:S(2)}, u32[]{:S(2)}) %all-to-all-start.2) | async-done | bytes 33554464 | tf_op jit(solution)/shard_map/all_to_all | solution.py:23
  6055.2 105.7 %fusion.1 = f32[8192,2752]{0,1:T(8,128)} fusion(bf16[8192,2048]{1,0:T(8,128)(2,1)} %bitcast.47, pred[]{:T(512)} %get-tuple-element.74, bf16[2,2048,2752]{1,2,0:T(8,128)(2,1)} %get-tuple-element.79, s32[]{:T(128)} %bitcast.50, bf16[2,1,2048,2752]{2,3,1,0:T(8,128)(2,1)} %param.12), kind=kOutput, calls=%fused_computation.42 | convolution fusion | flops 92347432960 | bytes 146277376 | tf_op jit(solution)/shard_map/scd,sdf->scf/dot_general | solution.py:24
  6160.9 261.4 %multiply_convert_fusion = bf16[8192,2752]{0,1:T(8,128)(2,1)} fusion(f32[8192,2752]{0,1:T(8,128)} %fusion.1, bf16[8192,2048]{1,0:T(8,128)(2,1)} %bitcast.47, pred[]{:T(512)} %get-tuple-element.74, bf16[2,2048,2752]{1,2,0:T(8,128)(2,1)} %get-tuple-element.80, s32[]{:T(128)} %bitcast.50, bf16[2,1,2048,2752]{2,3,1,0:T(8,128)(2,1)} %param.13), kind=kOutput, calls=%fused_computation.12 | convolution fusion | flops 92482699264 | bytes 191366144 | tf_op jit(solution)/shard_map/scd,sdf->scf/dot_general | solution.py:25
  6422.3 110.2 %convolution_bitcast_fusion = f32[1,8192,2048]{2,1,0:T(8,128)} fusion(bf16[8192,2752]{0,1:T(8,128)(2,1)} %multiply_convert_fusion, pred[]{:T(512)} %get-tuple-element.74, bf16[2,2752,2048]{2,1,0:T(8,128)(2,1)} %all-reduce.8.cloned.1.call-done, s32[]{:T(128)} %bitcast.50, bf16[2,1,2752,2048]{3,2,1,0:T(8,128)(2,1)} %param.14), kind=kOutput, calls=%fused_computation.14 | convolution fusion | flops 92347432960 | bytes 134743040 | tf_op jit(solution)/shard_map/scf,sfd->scd/dot_general | solution.py:27
  6532.5 1500.5 %all-reduce.12 = bf16[1,8192,2048]{2,1,0:T(8,128)(2,1)} all-reduce(f32[1,8192,2048]{2,1,0:T(8,128)} %convolution_bitcast_fusion), channel_id=1, replica_groups=mesh['rep'=1,'tp'=2,'ep'=4] {'tp'}, use_global_device_ids=true, to_apply=%region_24.25 | all-reduce | flops 16777216 | bytes 100663296 | tf_op jit(solution)/shard_map/psum | solution.py:28
  8033.0 56.6 copy.47
  8089.6 196.0 %reduce.38 = bf16[8192,2048]{1,0:T(8,128)(2,1)} reduce(bf16[8192,1,1,2048]{3,2,1,0:T(2,128)(2,1)} %bitcast.210, bf16[]{:T(256)} %broadcast.635), dimensions={1,2}, to_apply=%bitcast.210.reduce_sub_computation | reduce | bytes 67108864
  8285.5 50.4 reshape.871
  8335.9 10.1 all-to-all-start.3
  8347.9 45.4 bitcast_select_fusion.3
  8393.4 23.4 pad_maximum_fusion
  8416.9 16.3 pad_maximum_fusion.1
  8433.3 18.4 bitcast_select_fusion.1
  8451.6 19.4 pad_maximum_fusion.2
  8471.0 237.4 %all-to-all-done.3 = bf16[4,2,2097152]{2,1,0:T(2,128)(2,1)} async-done(((bf16[4,2,2097152]{2,1,0:T(2,128)(2,1)}), bf16[4,2,2097152]{2,1,0:T(2,128)(2,1)}, u32[]{:S(2)}, u32[]{:S(2)}) %all-to-all-start.3) | async-done | bytes 33554464 | tf_op jit(solution)/shard_map/all_to_all | solution.py:29
  8708.4 74.1 reshape.872
  8782.5 41.1 copy.45
  8823.6 95.7 %gather_fusion.5 = bf16[4096,2048]{1,0:T(8,128)(2,1)} fusion(bf16[8192,2048]{1,0:T(8,128)(2,1)} %bitcast.215, s32[4096]{0:T(1024)S(1)} %copy-done.4), kind=kCustom, calls=%fused_computation.5 | custom fusion | bytes 33570816 | tf_op jit(solution)/shard_map/gather | solution.py:30
  8919.3 35.3 reshape.702
  8954.6 56.3 multiply_reduce_fusion
  9011.0 12.0 add_convert_fusion
  (115 shorter events, 74.8 us)
Async XLA Ops:
  7.2 2285.7 %all-reduce.10.cloned.1.call-start = ((), (), s32[]{:S(2)}) async-start(), calls=%async_computation.5 | async-start | bytes 225443840 | tf_op jit(solution)/shard_map/psum | solution.py:67
  7.2 21.9 copy-start.1
  38.2 13.2 copy-start.18
  51.4 30.2 copy-start.16
  103.1 0.8 copy-start.11
  103.1 3.0 copy-start.20
  103.1 4.1 copy-start.14
  122.3 82.3 copy-start.13
  122.5 0.6 copy-start.7
  204.6 733.9 %all-to-all-start = ((bf16[4,1,2048,2048]{3,2,1,0:T(8,128)(2,1)}), bf16[4,1,2048,2048]{3,2,1,0:T(8,128)(2,1)}, u32[]{:S(2)}, u32[]{:S(2)}) async-start(bf16[4,1,2048,2048]{3,2,1,0:T(8,128)(2,1)} %bitcast.219), calls=%async_computation | async-start | bytes 67108864 | tf_op jit(solution)/shard_map/all_to_all | solution.py:23
  4586.3 9.9 copy-start.12
  4586.3 10.8 copy-start.6
  4586.3 11.9 copy-start
  4586.3 12.6 copy-start.19
  4586.3 34.6 copy-start.8
  4586.3 372.3 %all-to-all-start.1 = ((bf16[4,2,2097152]{2,1,0:T(2,128)(2,1)}), bf16[4,2,2097152]{2,1,0:T(2,128)(2,1)}, u32[]{:S(2)}, u32[]{:S(2)}) async-start(bf16[4,2,2097152]{2,1,0:T(2,128)(2,1)} %reshape.869), calls=%async_computation.1 | async-start | bytes 67108864 | tf_op jit(solution)/shard_map/all_to_all | solution.py:29
  4605.2 15.7 copy-start.9
  5347.6 10.0 copy-start.17
  5347.6 707.6 %all-to-all-start.2 = ((bf16[4,1,2048,2048]{3,2,1,0:T(8,128)(2,1)}), bf16[4,1,2048,2048]{3,2,1,0:T(8,128)(2,1)}, u32[]{:S(2)}, u32[]{:S(2)}) async-start(bf16[4,1,2048,2048]{3,2,1,0:T(8,128)(2,1)} %bitcast.218), calls=%async_computation.2 | async-start | bytes 67108864 | tf_op jit(solution)/shard_map/all_to_all | solution.py:23
  5357.5 1064.8 %all-reduce.8.cloned.1.call-start = ((), (), s32[]{:S(2)}) async-start(), calls=%async_computation.4 | async-start | bytes 45088768 | tf_op jit(solution)/shard_map/psum | solution.py:67
  5357.6 14.0 copy-start.15
  8335.9 10.1 copy-start.5
  8335.9 11.4 copy-start.10
  8335.9 372.5 %all-to-all-start.3 = ((bf16[4,2,2097152]{2,1,0:T(2,128)(2,1)}), bf16[4,2,2097152]{2,1,0:T(2,128)(2,1)}, u32[]{:S(2)}, u32[]{:S(2)}) async-start(bf16[4,2,2097152]{2,1,0:T(2,128)(2,1)} %reshape.871), calls=%async_computation.3 | async-start | bytes 67108864 | tf_op jit(solution)/shard_map/all_to_all | solution.py:29
  8393.4 23.5 copy-start.2
  8393.4 39.8 slice-start
  8393.4 39.8 slice-start.1
  8393.4 39.8 slice-start.2
  8416.9 16.4 slice-start.3
  8416.9 16.4 slice-start.4
  8416.9 16.4 slice-start.5
  8782.5 41.1 copy-start.4
  8919.3 35.3 copy-start.3
Sparse Core Ops, SparseCore 0:
  103.3 2189.5 all-reduce.9
  5371.7 711.4 all-reduce.7
where the time goes:
time: 9040 us; the launch traced here: 9030 us
  waiting for transfers between devices  3330 us (37%)
  blocking collectives  3010 us (33%)
  matrix products  954 us (11%)
  local copies, waits for them, and re-layouts  942 us (10%)
  other arithmetic  731 us (8%)
    psum x2, blocking collectives, moe_layer(): expert_out = lax.psum(part_out, 'tp').astype(jnp.bfloat16)  3010 us
    all_to_all x2, waiting for transfers between devices, moe_layer(): lax.all_to_all(send_rows, 'ep', 0, 2, tiled=True)  1400 us
    psum x2, waiting for transfers between devices, device_step(): lax.psum(outgoing_rows(weights, move_src[layer_idx], my_rank, local_slots...  1350 us
    all_to_all x2, waiting for transfers between devices, moe_layer(): lax.all_to_all(expert_out.reshape(1, local_slots, group_size * capacity,...  575 us
    dot_general x2, matrix products, moe_layer(): jnp.einsum('scd,sdf->scf', recv_rows, w_up, preferred_element_type=jnp.fl...  522 us
    unnamed x5, other arithmetic  392 us
    unnamed x61, local copies, waits for them, and re-layouts  338 us
    dot_general x2, matrix products, moe_layer(): jnp.einsum('scf,sfd->scd', hidden_act, w_down, preferred_element_type=jnp...  220 us
  transfers between devices with their start and end apart: 6, of which 5 were waited for; matrix products, arithmetic and copies ran while one was open for 7% of the time, Pallas kernels for 0%

commit v1 on v0

v1 whole, which is shorter than its diff:
```python
import jax
import jax.numpy as jnp
from jax import lax
from jax.experimental import pallas as pl
from jax.experimental.pallas import tpu as pltpu
from jax.sharding import PartitionSpec as P


HALF_CHUNK = 256
WEIGHT_CHUNKS = 8
FFN_TILES = 4
INSTALL_TILES = 4


def running_count(mask):
    length = mask.shape[-1]
    blocks = mask.reshape(mask.shape[:-1] + (length // 128, 128)).astype(jnp.bfloat16)
    upper = (jnp.arange(128)[:, None] <= jnp.arange(128)[None, :]).astype(jnp.bfloat16)
    inner = jnp.einsum('...bk,kn->...bn', blocks, upper, preferred_element_type=jnp.float32)
    strict = (jnp.arange(length // 128)[:, None] < jnp.arange(length // 128)[None, :]).astype(jnp.bfloat16)
    before = jnp.einsum('...b,bn->...n', inner[..., -1].astype(jnp.bfloat16), strict, preferred_element_type=jnp.float32)
    return (inner + before[..., None]).reshape(mask.shape).astype(jnp.int32)


def mlp_kernel(rows_ref, gate_ref, up_ref, down_ref, part_ref):
    tile = pl.program_id(0)
    rows = rows_ref[...]
    across = (((1,), (1,)), ((), ()))
    gate_acc = lax.dot_general(rows, gate_ref[0, 0], across, preferred_element_type=jnp.float32)
    up_acc = lax.dot_general(rows, up_ref[0, 0], across, preferred_element_type=jnp.float32)
    act = (jax.nn.silu(gate_acc) * up_acc).astype(jnp.bfloat16)
    part = jnp.dot(act, down_ref[0, 0], preferred_element_type=jnp.float32)

    @pl.when(tile == 0)
    def _():
        part_ref[...] = part

    @pl.when(tile != 0)
    def _():
        part_ref[...] += part


def expert_mlp(rows, gate_t, up_t, down, layer):
    count, width = rows.shape
    columns = down.shape[2]
    tile = columns // FFN_TILES
    weight_spec = pl.BlockSpec((1, 1, tile, width), lambda f: (layer, 0, f, 0))
    row_block = pl.BlockSpec((count, width), lambda f: (0, 0))
    return pl.pallas_call(
        mlp_kernel,
        grid=(FFN_TILES,),
        in_specs=[row_block, weight_spec, weight_spec, weight_spec],
        out_specs=row_block,
        out_shape=jax.ShapeDtypeStruct((count, width), jnp.float32),
        cost_estimate=pl.CostEstimate(flops=6 * count * width * columns, bytes_accessed=6 * width * columns + 8 * count * width, transcendentals=count * columns),
    )(rows, gate_t, up_t, down)


def install_kernel(flags_ref, own_ref, first_ref, back_ref, *refs):
    out_ref = refs[-1]
    tile = pl.program_id(0)
    moved = flags_ref[0] == 1
    from_first = (tile // INSTALL_TILES) == flags_ref[1]

    @pl.when(jnp.logical_not(moved))
    def _():
        out_ref[0, 0] = own_ref[0, 0]

    @pl.when(jnp.logical_and(moved, from_first))
    def _():
        out_ref[0, 0] = first_ref[...]

    @pl.when(jnp.logical_and(moved, jnp.logical_not(from_first)))
    def _():
        out_ref[0, 0] = back_ref[...]


def install(flags, own, first, back, layer, earlier):
    _, _, rows, width = own.shape
    tile = rows // 2 // INSTALL_TILES
    block = (1, 1, tile, width)

    def own_map(t, flags_ref):
        return (layer, 0, jnp.where(flags_ref[0] == 1, 0, t), 0)

    def first_map(t, flags_ref):
        used = jnp.logical_and(flags_ref[0] == 1, (t // INSTALL_TILES) == flags_ref[1])
        return (jnp.where(used, t % INSTALL_TILES, 0), 0)

    def back_map(t, flags_ref):
        used = jnp.logical_and(flags_ref[0] == 1, (t // INSTALL_TILES) != flags_ref[1])
        return (jnp.where(used, t % INSTALL_TILES, 0), 0)

    in_specs = [pl.BlockSpec(block, own_map), pl.BlockSpec((tile, width), first_map), pl.BlockSpec((tile, width), back_map)]
    operands = [flags, own, first, back]
    aliases = {}
    if earlier is not None:
        in_specs.append(pl.BlockSpec(memory_space=pl.ANY))
        operands.append(earlier)
        aliases = {4: 0}
    return pl.pallas_call(
        install_kernel,
        grid_spec=pltpu.PrefetchScalarGridSpec(
            num_scalar_prefetch=1, grid=(2 * INSTALL_TILES,), in_specs=in_specs,
            out_specs=pl.BlockSpec(block, lambda t, flags_ref: (layer, 0, t, 0))),
        out_shape=jax.ShapeDtypeStruct(own.shape, own.dtype),
        input_output_aliases=aliases,
        cost_estimate=pl.CostEstimate(flops=200 * rows * width, bytes_accessed=4 * rows * width, transcendentals=0),
    )(*operands)


def solution(mesh):
    group_size = mesh.shape['ep']
    row_spec = P(('rep', 'ep'), None)
    layer_spec = P(None, ('rep', 'ep'), None)
    col_spec = P(None, ('rep', 'ep'), None, 'tp')
    down_spec = P(None, ('rep', 'ep'), 'tp', None)
    map_spec = P(None, None)

    def over_tp(arr):
        return lax.ppermute(arr, 'tp', [(0, 1), (1, 0)])

    def over_x(arr):
        return lax.ppermute(arr, 'ep', [(i, i ^ 2) for i in range(group_size)])

    def over_core(arr):
        return lax.ppermute(arr, 'ep', [(i, i ^ 1) for i in range(group_size)])

    def device_step(x_in, route_ids, gate_vals, w_gate, w_up, w_down, old_map, move_src, move_dst):
        tokens, width = x_in.shape
        layers = route_ids.shape[0]
        half = tokens // 2
        list_len = group_size * half
        max_chunks = list_len // HALF_CHUNK
        me = lax.axis_index('ep')
        tp = lax.axis_index('tp')
        core = me % 2
        gate_t, up_t = w_gate.swapaxes(2, 3), w_up.swapaxes(2, 3)
        experts = jnp.arange(group_size, dtype=jnp.int32)

        all_ids = lax.all_gather(route_ids, 'ep', axis=1, tiled=True)
        x_in, all_ids = lax.optimization_barrier((x_in, all_ids))
        ids6 = all_ids.reshape(layers, group_size, 2, half, 2)
        chosen = jnp.any(ids6[None] == experts[:, None, None, None, None, None], axis=-1)
        mask = chosen.transpose(1, 3, 0, 2, 4).reshape(layers, 2, group_size, list_len)
        counts = running_count(mask)
        rank = counts - 1
        trips = (jnp.max(counts[..., -1], axis=(1, 2)) + HALF_CHUNK - 1) // HALF_CHUNK

        def expert_lists(layer, my_expert):
            mine = lax.dynamic_index_in_dim(counts[layer], my_expert, axis=1, keepdims=False)
            slots = jnp.arange(list_len, dtype=jnp.int32)
            found = jnp.sum((mine[:, None, :] <= slots[None, :, None]).astype(jnp.int32), axis=-1)
            found = jnp.where(slots[None, :] < mine[:, -1:], found, slots[None, :])
            keep = lax.dynamic_index_in_dim(found, tp, 0, keepdims=False)
            send = lax.dynamic_index_in_dim(found, 1 - tp, 0, keepdims=False)
            return keep, send

        def layer_fn(layer, rows_all, index_of, hidden_half, buffer):
            slot_of = jnp.sum(jnp.where(old_map[layer][None, :] == experts[:, None], experts[None, :], 0), axis=1)
            my_expert = old_map[layer, me]
            keep_list, send_list = expert_lists(layer, my_expert)
            keep_list = index_of(keep_list, tp)
            send_list = index_of(send_list, 1 - tp)
            order = jnp.concatenate([keep_list.reshape(max_chunks, HALF_CHUNK), send_list.reshape(max_chunks, HALF_CHUNK)], axis=1)
            wg, wu, wd = w_gate[layer, 0].T, w_up[layer, 0].T, w_down[layer, 0]

            peer = move_dst[layer, 0] ^ move_dst[layer, 1]
            moved = jnp.any(move_dst[layer] == me)
            in_chip = peer == 1
            halves = [w.reshape(2, w.shape[0] // 2, w.shape[1]) for w in (wg, wu, wd)]
            own_part = [lax.dynamic_index_in_dim(w, core, 0, keepdims=False) for w in halves]
            other_part = [lax.dynamic_index_in_dim(w, 1 - core, 0, keepdims=False) for w in halves]
            from_core = [over_core(w) for w in other_part]
            outgoing = [jnp.where(moved, o, f).reshape(-1, 8, width) for o, f in zip(own_part, from_core)]
            steps = [-(-w.shape[0] // WEIGHT_CHUNKS) for w in outgoing]

            def compute(i):
                idx = lax.dynamic_index_in_dim(order, i, 0, keepdims=False)
                rows = rows_all.at[idx].get(mode='promise_in_bounds')
                part = expert_mlp(rows, gate_t, up_t, w_down, layer)
                return part[:HALF_CHUNK], part[HALF_CHUNK:]

            def put(buffer, i, pair, crossed):
                block = jnp.concatenate([pair, crossed], axis=0)[None]
                return lax.dynamic_update_slice(buffer, block, (jnp.maximum(i, 0), 0, 0, 0))

            def stages(i, carry):
                keep, send, rounded, pair, buffer = carry
                recv = over_tp(send)
                across = over_x(rounded)
                crossed = over_core(pair)
                new_keep, new_send = compute(i)
                buffer = put(buffer, i - 3, pair, crossed)
                return new_keep, new_send, (keep + recv).astype(jnp.bfloat16), jnp.stack([rounded, across]), buffer

            def plain(i, carry):
                return stages(i, carry)

            def with_weights(i, state):
                return with_swap(i, state)

            def with_swap(i, state):
                carry, incoming = state
                landed = []
                for out, inc, step in zip(outgoing, incoming, steps):
                    start = jnp.minimum((i - 1) * step, out.shape[0] - step)
                    piece = over_x(lax.dynamic_slice(out, (start, 0, 0), (step, 8, width)))
                    landed.append(lax.dynamic_update_slice(inc, piece, (start, 0, 0)))
                return stages(i, carry), tuple(landed)

            zero = jnp.zeros((HALF_CHUNK, width), jnp.bfloat16)
            first_keep, first_send = compute(0)
            carry = (first_keep, first_send, zero, jnp.zeros((2, HALF_CHUNK, width), jnp.bfloat16), buffer)
            trip = trips[layer]
            split = jnp.where(in_chip, 1, 1 + WEIGHT_CHUNKS)
            carry, incoming = lax.fori_loop(1, split, with_weights, (carry, tuple(jnp.zeros_like(o) for o in outgoing)))
            carry = lax.fori_loop(split, jnp.maximum(trip, split), plain, carry)
            trip = jnp.maximum(trip, split)
            incoming = [inc.reshape(-1, width) for inc in incoming]
            keep, send, rounded, pair, buffer = carry
            recv = over_tp(send)
            across = over_x(rounded)
            buffer = put(buffer, trip - 3, pair, over_core(pair))
            last = (keep + recv).astype(jnp.bfloat16)
            pair = jnp.stack([rounded, across])
            buffer = put(buffer, trip - 2, pair, over_core(pair))
            pair = jnp.stack([last, over_x(last)])
            buffer = put(buffer, trip - 1, pair, over_core(pair))

            my_ids = lax.dynamic_slice_in_dim(route_ids[layer], tp * half, half, 0)
            my_gates = lax.dynamic_slice_in_dim(gate_vals[layer], tp * half, half, 0)
            my_rank = lax.dynamic_slice(rank[layer], (tp, 0, me * half), (1, group_size, half))[0]
            pos = jnp.sum(jnp.where(my_ids[:, :, None] == experts, my_rank.T[:, None, :], 0), axis=-1)
            relative = slot_of[my_ids] ^ me
            place = (relative % 2) * 2 + relative // 2
            flat = ((pos // HALF_CHUNK) * 4 + place) * HALF_CHUNK + pos % HALF_CHUNK
            table = buffer.reshape(max_chunks * 4 * HALF_CHUNK, width)
            mixture = jnp.zeros((half, width), jnp.float32)
            for j in range(2):
                picked = table.at[flat[:, j]].get(mode='promise_in_bounds')
                mixture = mixture + my_gates[:, j:j + 1] * picked.astype(jnp.float32)
            hidden_next = (hidden_half.astype(jnp.float32) + mixture).astype(jnp.bfloat16)

            back = [over_core(jnp.where(in_chip, o, inc)) for o, inc in zip(own_part, incoming)]
            first = [jnp.where(in_chip, f, inc) for f, inc in zip(from_core, incoming)]
            flags = jnp.stack([moved.astype(jnp.int32), core.astype(jnp.int32)])
            new = (flags, first, back)
            return hidden_next, new, buffer

        relay = 688
        x_half = x_in.reshape(2, half, width)
        my_half = lax.dynamic_index_in_dim(x_half, tp, 0, keepdims=False)
        first = over_x(my_half[:relay])
        rest = over_x(jnp.concatenate([x_half[0, relay:], x_half[1, relay:]], axis=0))
        relayed = over_tp(first)
        sides = jnp.stack([first, relayed])
        low = lax.dynamic_index_in_dim(sides, tp, 0, keepdims=False)
        high = lax.dynamic_index_in_dim(sides, 1 - tp, 0, keepdims=False)
        mid = half - relay
        far = jnp.concatenate([low, rest[:mid], high, rest[mid:]], axis=0)
        near = over_core(x_in)
        far_core = over_core(far)
        rows_all = jnp.concatenate([x_in, near, far, far_core], axis=0)

        def index0(pos, hf):
            home = pos // half
            return (home ^ me) * tokens + hf * half + pos % half

        buffer = jnp.zeros((max_chunks, 4, HALF_CHUNK, width), jnp.bfloat16)
        rows_all, buffer = lax.optimization_barrier((rows_all, buffer))
        h1, (flags, first, back), buffer = layer_fn(0, rows_all, index0, my_half, buffer)
        wholes = (gate_t, up_t, w_down)
        made = [install(flags, w, f, b, 0, None) for w, f, b in zip(wholes, first, back)]

        by_x = over_x(h1)
        by_y = over_tp(h1)
        quarter = half // 2
        xy_low = over_tp(by_x[:quarter])
        xy_high = over_x(by_y[quarter:])
        mine4 = jnp.concatenate([h1, by_x, by_y, xy_low, xy_high], axis=0)
        core4 = over_core(mine4)
        rows_all = jnp.concatenate([mine4, core4], axis=0)

        def index1(pos, hf):
            relative = (pos // half) ^ me
            block = (relative % 2) * 4 + (hf ^ tp) * 2 + relative // 2
            return block * half + pos % half

        h2, (flags, first, back), _ = layer_fn(1, rows_all, index1, h1, buffer)
        h2, made = lax.optimization_barrier((h2, made))
        other = over_tp(h2)
        y_out = jnp.concatenate([jnp.where(tp == 0, h2, other), jnp.where(tp == 0, other, h2)], axis=0)
        new_gate, new_up, new_down = [install(flags, w, f, b, 1, m) for w, f, b, m in zip(wholes, first, back, made)]
        return y_out, new_gate.swapaxes(2, 3), new_up.swapaxes(2, 3), new_down

    return jax.shard_map(device_step, mesh=mesh, in_specs=(row_spec, layer_spec, layer_spec, col_spec, col_spec, down_spec, map_spec, map_spec, map_spec), out_specs=(row_spec, col_spec, col_spec, down_spec), check_vma=False)
```

time: 9040 us -> 2560 us (0.28)
  blocking collectives: 3010 us -> 10.2 us
  waiting for transfers between devices: 3330 us -> 565 us
  matrix products: 954 us -> 0.3 us
  Pallas kernels: 0 us -> 725 us
  other arithmetic: 731 us -> 364 us
  local copies, waits for them, and re-layouts: 942 us -> 761 us
    psum x2 -> x0, blocking collectives: 3010 us -> none  [moe_layer(): expert_out = lax.psum(part_out, 'tp').astype(jnp.bfloat16)]
    all_to_all x4 -> x0, waiting for transfers between devices: 1980 us -> none  [the longest x2 1400 us: moe_layer(): lax.all_to_all(send_rows, 'ep', 0, 2, tiled=True)]
    psum x2 -> x0, waiting for transfers between devices: 1350 us -> none  [device_step(): lax.psum(outgoing_rows(weights, move_src[layer_idx], my_rank, local_slots...]
    dot_general x6 -> x2, matrix products: 954 us -> 0.3 us  [the longest x1 0.18 us: running_count(): jnp.einsum('...bk,kn->...bn', blocks, upper, preferred_element_type=jnp.f...]
    pallas_call x0 -> x28, Pallas kernels: none -> 725 us  [the longest x22 651 us: expert_mlp(): pl.pallas_call(mlp_kernel, grid=(FFN_TILES,), in_specs=[row_block, weight...]
    ppermute x0 -> x143, waiting for transfers between devices: none -> 565 us  [the longest x76 372 us: over_x(): return lax.ppermute(arr, 'ep', [(i, i ^ 2) for i in range(group_size)])]
    unnamed x5 -> x11, other arithmetic: 392 us -> 14.8 us
    unnamed x61 -> x111, local copies, waits for them, and re-layouts: 338 us -> 37.9 us
  transfers between devices with their start and end apart: 6 -> 143, of which waited for: 5 -> 30; matrix products, arithmetic and copies ran while one was open for 7% -> 34% of each run, Pallas kernels for 0% -> 26%
where the time goes in v1:
time: 2560 us; the launch traced here: 2540 us
  local copies, waits for them, and re-layouts  761 us (30%)
  Pallas kernels  725 us (28%)
  waiting for transfers between devices  565 us (22%)
  other arithmetic  364 us (14%)
  starting transfers between devices  105 us (4%)
    pallas_call x22, Pallas kernels, expert_mlp(): pl.pallas_call(mlp_kernel, grid=(FFN_TILES,), in_specs=[row_block, weight...  651 us
    ppermute x76, waiting for transfers between devices, over_x(): return lax.ppermute(arr, 'ep', [(i, i ^ 2) for i in range(group_size)])  372 us
    ppermute x26, waiting for transfers between devices, over_tp(): return lax.ppermute(arr, 'tp', [(0, 1), (1, 0)])  171 us
    gather x22, local copies, waits for them, and re-layouts, compute(): rows = rows_all.at[idx].get(mode='promise_in_bounds')  147 us
    dynamic_update_slice x48, local copies, waits for them, and re-layouts, with_swap(): landed.append(lax.dynamic_update_slice(inc, piece, (start, 0, 0)))  101 us
    dynamic_slice x48, local copies, waits for them, and re-layouts, with_swap(): piece = over_x(lax.dynamic_slice(out, (start, 0, 0), (step, 8, width)))  98.9 us
    gather x4, local copies, waits for them, and re-layouts, layer_fn(): picked = table.at[flat[:, j]].get(mode='promise_in_bounds')  97.4 us
    another operation x30, local copies, waits for them, and re-layouts  85.7 us
  transfers between devices with their start and end apart: 143, of which 30 were waited for; matrix products, arithmetic and copies ran while one was open for 34% of the time, Pallas kernels for 26%

profile of v1, /device:TPU:0, one launch (start us, length us, event | category | flops | bytes accessed | tf_op | source)
XLA Modules:
  0.0 2542.0 jit_solution(3311251343040045364)
XLA Ops:
  20.3 16.1 fusion.96
  58.2 18.7 fusion.94
  108.9 20.0 convert_reduce_fusion
  137.8 23.9 collective-permute-done.20
  176.4 20.4 convert_reduce_fusion.1
  247.0 29.5 %shard_map.111 = f32[512,2048]{1,0:T(8,128)} custom-call(bf16[512,2048]{1,0:T(8,128)(2,1)} %gather_fusion.4, bf16[2,1,2752,2048]{3,2,1,0:T(8,128)(2,1)} %bitcast.334, bf16[2,1,2752,2048]{3,2,1,0:T(8,128)(2,1)} %bitcast.330, bf16[2,1,2752,2048]{3,2,1,0:T(8,128)(2,1)} %own_ref.3), custom_call_target="tpu_custom_call" | custom-call | flops 17314086912 | bytes 42205184 | tf_op jit(solution)/shard_map/pallas_call | solution.py:49
  280.5 21.3 broadcast_in_dim.126
  313.0 644.7 %while.92 = (s32[]{:T(128)}, f32[256,2048]{1,0:T(8,128)S(1)}, f32[256,2048]{1,0:T(8,128)}, bf16[256,2048]{1,0:T(8,128)(2,1)S(1)}, bf16[2,256,2048]{2,1,0:T(8,128...) while((s32[]{:T(128)}, f32[256,2048]{1,0:T(8,128)S(1)}, ...), condition=%wide.region_4.5_spmd, body=%wide.region_3.4_spmd.sunk | while | flops 17324574720 | bytes 140260032 | solution.py:217
  331.5 29.6 %body.16 = f32[512,2048]{1,0:T(8,128)} custom-call(bf16[512,2048]{1,0:T(8,128)(2,1)} %gather_fusion, bf16[2,1,2752,2048]{3,2,1,0:T(8,128)(2,1)} %get-tuple-element.1475.gate_ref, bf16[2,1,2752,2048]{3,2,1,0:T(8,128)(2,1)} %get-tuple-element.1476.up_ref, bf16[2,1,2752,2048]{3,2,1,0:T(8,128)(2,1)} %get-tuple-element.1477.down_ref), custom_call_target="tpu_custom_call" | custom-call | flops 17314086912 | bytes 42205184 | tf_op jit(solution)/shard_map/while/body/pallas_call | solution.py:49
  413.8 29.6 %body.16 = f32[512,2048]{1,0:T(8,128)} custom-call(bf16[512,2048]{1,0:T(8,128)(2,1)} %gather_fusion, bf16[2,1,2752,2048]{3,2,1,0:T(8,128)(2,1)} %get-tuple-element.1475.gate_ref, bf16[2,1,2752,2048]{3,2,1,0:T(8,128)(2,1)} %get-tuple-element.1476.up_ref, bf16[2,1,2752,2048]{3,2,1,0:T(8,128)(2,1)} %get-tuple-element.1477.down_ref), custom_call_target="tpu_custom_call" | custom-call | flops 17314086912 | bytes 42205184 | tf_op jit(solution)/shard_map/while/body/pallas_call | solution.py:49
  452.9 15.8 collective-permute-done.1
  496.2 29.6 %body.16 = f32[512,2048]{1,0:T(8,128)} custom-call(bf16[512,2048]{1,0:T(8,128)(2,1)} %gather_fusion, bf16[2,1,2752,2048]{3,2,1,0:T(8,128)(2,1)} %get-tuple-element.1475.gate_ref, bf16[2,1,2752,2048]{3,2,1,0:T(8,128)(2,1)} %get-tuple-element.1476.up_ref, bf16[2,1,2752,2048]{3,2,1,0:T(8,128)(2,1)} %get-tuple-element.1477.down_ref), custom_call_target="tpu_custom_call" | custom-call | flops 17314086912 | bytes 42205184 | tf_op jit(solution)/shard_map/while/body/pallas_call | solution.py:49
  578.3 29.6 %body.16 = f32[512,2048]{1,0:T(8,128)} custom-call(bf16[512,2048]{1,0:T(8,128)(2,1)} %gather_fusion, bf16[2,1,2752,2048]{3,2,1,0:T(8,128)(2,1)} %get-tuple-element.1475.gate_ref, bf16[2,1,2752,2048]{3,2,1,0:T(8,128)(2,1)} %get-tuple-element.1476.up_ref, bf16[2,1,2752,2048]{3,2,1,0:T(8,128)(2,1)} %get-tuple-element.1477.down_ref), custom_call_target="tpu_custom_call" | custom-call | flops 17314086912 | bytes 42205184 | tf_op jit(solution)/shard_map/while/body/pallas_call | solution.py:49
  659.6 29.6 %body.16 = f32[512,2048]{1,0:T(8,128)} custom-call(bf16[512,2048]{1,0:T(8,128)(2,1)} %gather_fusion, bf16[2,1,2752,2048]{3,2,1,0:T(8,128)(2,1)} %get-tuple-element.1475.gate_ref, bf16[2,1,2752,2048]{3,2,1,0:T(8,128)(2,1)} %get-tuple-element.1476.up_ref, bf16[2,1,2752,2048]{3,2,1,0:T(8,128)(2,1)} %get-tuple-element.1477.down_ref), custom_call_target="tpu_custom_call" | custom-call | flops 17314086912 | bytes 42205184 | tf_op jit(solution)/shard_map/while/body/pallas_call | solution.py:49
  740.1 29.6 %body.16 = f32[512,2048]{1,0:T(8,128)} custom-call(bf16[512,2048]{1,0:T(8,128)(2,1)} %gather_fusion, bf16[2,1,2752,2048]{3,2,1,0:T(8,128)(2,1)} %get-tuple-element.1475.gate_ref, bf16[2,1,2752,2048]{3,2,1,0:T(8,128)(2,1)} %get-tuple-element.1476.up_ref, bf16[2,1,2752,2048]{3,2,1,0:T(8,128)(2,1)} %get-tuple-element.1477.down_ref), custom_call_target="tpu_custom_call" | custom-call | flops 17314086912 | bytes 42205184 | tf_op jit(solution)/shard_map/while/body/pallas_call | solution.py:49
  819.6 29.6 %body.16 = f32[512,2048]{1,0:T(8,128)} custom-call(bf16[512,2048]{1,0:T(8,128)(2,1)} %gather_fusion, bf16[2,1,2752,2048]{3,2,1,0:T(8,128)(2,1)} %get-tuple-element.1475.gate_ref, bf16[2,1,2752,2048]{3,2,1,0:T(8,128)(2,1)} %get-tuple-element.1476.up_ref, bf16[2,1,2752,2048]{3,2,1,0:T(8,128)(2,1)} %get-tuple-element.1477.down_ref), custom_call_target="tpu_custom_call" | custom-call | flops 17314086912 | bytes 42205184 | tf_op jit(solution)/shard_map/while/body/pallas_call | solution.py:49
  898.3 29.6 %body.16 = f32[512,2048]{1,0:T(8,128)} custom-call(bf16[512,2048]{1,0:T(8,128)(2,1)} %gather_fusion, bf16[2,1,2752,2048]{3,2,1,0:T(8,128)(2,1)} %get-tuple-element.1475.gate_ref, bf16[2,1,2752,2048]{3,2,1,0:T(8,128)(2,1)} %get-tuple-element.1476.up_ref, bf16[2,1,2752,2048]{3,2,1,0:T(8,128)(2,1)} %get-tuple-element.1477.down_ref), custom_call_target="tpu_custom_call" | custom-call | flops 17314086912 | bytes 42205184 | tf_op jit(solution)/shard_map/while/body/pallas_call | solution.py:49
  957.7 110.9 %while.93 = (s32[]{:T(128)}, f32[256,2048]{1,0:T(8,128)S(1)}, f32[256,2048]{1,0:T(8,128)}, bf16[256,2048]{1,0:T(8,128)(2,1)S(1)}, bf16[2,256,2048]{2,1,0:T(8,128...) while((s32[]{:T(128)}, f32[256,2048]{1,0:T(8,128)S(1)}, ...), condition=%wide.region_7.8_spmd, body=%wide.region_6.7_spmd.sunk | while | flops 17324574720 | bytes 114569592 | solution.py:218
  970.8 29.5 %body.17 = f32[512,2048]{1,0:T(8,128)} custom-call(bf16[512,2048]{1,0:T(8,128)(2,1)} %gather_fusion.1, bf16[2,1,2752,2048]{3,2,1,0:T(8,128)(2,1)} %get-tuple-element.1530.gate_ref, bf16[2,1,2752,2048]{3,2,1,0:T(8,128)(2,1)} %get-tuple-element.1531.up_ref, bf16[2,1,2752,2048]{3,2,1,0:T(8,128)(2,1)} %get-tuple-element.1532.down_ref), custom_call_target="tpu_custom_call" | custom-call | flops 17314086912 | bytes 42205184 | tf_op jit(solution)/shard_map/while/body/pallas_call | solution.py:49
  1022.4 29.5 %body.17 = f32[512,2048]{1,0:T(8,128)} custom-call(bf16[512,2048]{1,0:T(8,128)(2,1)} %gather_fusion.1, bf16[2,1,2752,2048]{3,2,1,0:T(8,128)(2,1)} %get-tuple-element.1530.gate_ref, bf16[2,1,2752,2048]{3,2,1,0:T(8,128)(2,1)} %get-tuple-element.1531.up_ref, bf16[2,1,2752,2048]{3,2,1,0:T(8,128)(2,1)} %get-tuple-element.1532.down_ref), custom_call_target="tpu_custom_call" | custom-call | flops 17314086912 | bytes 42205184 | tf_op jit(solution)/shard_map/while/body/pallas_call | solution.py:49
  1069.6 46.2 %collective-permute-done.29 = f32[256,2048]{1,0:T(8,128)S(1)} collective-permute-done((f32[256,2048]{1,0:T(8,128)}, f32[256,2048]{1,0:T(8,128)S(1)}, u32[]{:S(2)}, u32[]{:S(2)}) %collective-permute-start.29) | collective-permute-done | bytes 2097184 | tf_op jit(solution)/shard_map/ppermute | solution.py:121
  1121.2 19.7 collective-permute-done.30
  1160.3 24.4 gather_fusion.5
  1184.6 24.3 gather_fusion.6
  1216.9 92.2 %collective-permute-done.32 = bf16[1024,2048]{1,0:T(8,128)(2,1)S(1)} collective-permute-done((bf16[1024,2048]{1,0:T(8,128)(2,1)S(1)}, bf16[1024,2048]{1,0:T(8,128)(2,1)S(1)}, u32[]{:S(2)}, u32[]{:S(2)}) %collective-permute-start.32) | collective-permute-done | bytes 4194336 | tf_op jit(solution)/shard_map/ppermute | solution.py:124
  1324.9 33.0 %collective-permute-done.34 = bf16[512,2048]{1,0:T(8,128)(2,1)S(1)} collective-permute-done((bf16[512,2048]{1,0:T(8,128)(2,1)}, bf16[512,2048]{1,0:T(8,128)(2,1)S(1)}, u32[]{:S(2)}, u32[]{:S(2)}) %collective-permute-start.34) | collective-permute-done | bytes 2097184 | tf_op jit(solution)/shard_map/ppermute | solution.py:121
  1378.1 18.4 collective-permute-done.39
  1446.8 29.6 %shard_map.112 = f32[512,2048]{1,0:T(8,128)} custom-call(bf16[512,2048]{1,0:T(8,128)(2,1)} %gather_fusion.7, bf16[2,1,2752,2048]{3,2,1,0:T(8,128)(2,1)} %get-tuple-element.1672, bf16[2,1,2752,2048]{3,2,1,0:T(8,128)(2,1)} %get-tuple-element.1668, bf16[2,1,2752,2048]{3,2,1,0:T(8,128)(2,1)} %get-tuple-element.1664), custom_call_target="tpu_custom_call" | custom-call | flops 17314086912 | bytes 42205184 | tf_op jit(solution)/shard_map/pallas_call | solution.py:49
  1491.6 654.6 %while.94 = (s32[]{:T(128)}, f32[256,2048]{1,0:T(8,128)S(1)}, f32[256,2048]{1,0:T(8,128)}, bf16[256,2048]{1,0:T(8,128)(2,1)S(1)}, bf16[2,256,2048]{2,1,0:T(8,128...) while((s32[]{:T(128)}, f32[256,2048]{1,0:T(8,128)S(1)}, ...), condition=%wide.region_13.14_spmd, body=%wide.region_12.13_spmd.sunk | while | flops 17324574720 | bytes 140260032 | solution.py:217
  1509.2 29.7 %body.18 = f32[512,2048]{1,0:T(8,128)} custom-call(bf16[512,2048]{1,0:T(8,128)(2,1)} %gather_fusion.2, bf16[2,1,2752,2048]{3,2,1,0:T(8,128)(2,1)} %get-tuple-element.1601.gate_ref, bf16[2,1,2752,2048]{3,2,1,0:T(8,128)(2,1)} %get-tuple-element.1602.up_ref, bf16[2,1,2752,2048]{3,2,1,0:T(8,128)(2,1)} %get-tuple-element.1603.down_ref), custom_call_target="tpu_custom_call" | custom-call | flops 17314086912 | bytes 42205184 | tf_op jit(solution)/shard_map/while/body/pallas_call | solution.py:49
  1590.8 29.7 %body.18 = f32[512,2048]{1,0:T(8,128)} custom-call(bf16[512,2048]{1,0:T(8,128)(2,1)} %gather_fusion.2, bf16[2,1,2752,2048]{3,2,1,0:T(8,128)(2,1)} %get-tuple-element.1601.gate_ref, bf16[2,1,2752,2048]{3,2,1,0:T(8,128)(2,1)} %get-tuple-element.1602.up_ref, bf16[2,1,2752,2048]{3,2,1,0:T(8,128)(2,1)} %get-tuple-element.1603.down_ref), custom_call_target="tpu_custom_call" | custom-call | flops 17314086912 | bytes 42205184 | tf_op jit(solution)/shard_map/while/body/pallas_call | solution.py:49
  1630.6 16.2 collective-permute-done.10
  1673.5 29.7 %body.18 = f32[512,2048]{1,0:T(8,128)} custom-call(bf16[512,2048]{1,0:T(8,128)(2,1)} %gather_fusion.2, bf16[2,1,2752,2048]{3,2,1,0:T(8,128)(2,1)} %get-tuple-element.1601.gate_ref, bf16[2,1,2752,2048]{3,2,1,0:T(8,128)(2,1)} %get-tuple-element.1602.up_ref, bf16[2,1,2752,2048]{3,2,1,0:T(8,128)(2,1)} %get-tuple-element.1603.down_ref), custom_call_target="tpu_custom_call" | custom-call | flops 17314086912 | bytes 42205184 | tf_op jit(solution)/shard_map/while/body/pallas_call | solution.py:49
  1712.7 18.0 collective-permute-done.10
  1757.3 29.7 %body.18 = f32[512,2048]{1,0:T(8,128)} custom-call(bf16[512,2048]{1,0:T(8,128)(2,1)} %gather_fusion.2, bf16[2,1,2752,2048]{3,2,1,0:T(8,128)(2,1)} %get-tuple-element.1601.gate_ref, bf16[2,1,2752,2048]{3,2,1,0:T(8,128)(2,1)} %get-tuple-element.1602.up_ref, bf16[2,1,2752,2048]{3,2,1,0:T(8,128)(2,1)} %get-tuple-element.1603.down_ref), custom_call_target="tpu_custom_call" | custom-call | flops 17314086912 | bytes 42205184 | tf_op jit(solution)/shard_map/while/body/pallas_call | solution.py:49
  1796.5 17.1 collective-permute-done.10
  1840.3 29.7 %body.18 = f32[512,2048]{1,0:T(8,128)} custom-call(bf16[512,2048]{1,0:T(8,128)(2,1)} %gather_fusion.2, bf16[2,1,2752,2048]{3,2,1,0:T(8,128)(2,1)} %get-tuple-element.1601.gate_ref, bf16[2,1,2752,2048]{3,2,1,0:T(8,128)(2,1)} %get-tuple-element.1602.up_ref, bf16[2,1,2752,2048]{3,2,1,0:T(8,128)(2,1)} %get-tuple-element.1603.down_ref), custom_call_target="tpu_custom_call" | custom-call | flops 17314086912 | bytes 42205184 | tf_op jit(solution)/shard_map/while/body/pallas_call | solution.py:49
  1879.4 16.2 collective-permute-done.10
  1922.4 29.7 %body.18 = f32[512,2048]{1,0:T(8,128)} custom-call(bf16[512,2048]{1,0:T(8,128)(2,1)} %gather_fusion.2, bf16[2,1,2752,2048]{3,2,1,0:T(8,128)(2,1)} %get-tuple-element.1601.gate_ref, bf16[2,1,2752,2048]{3,2,1,0:T(8,128)(2,1)} %get-tuple-element.1602.up_ref, bf16[2,1,2752,2048]{3,2,1,0:T(8,128)(2,1)} %get-tuple-element.1603.down_ref), custom_call_target="tpu_custom_call" | custom-call | flops 17314086912 | bytes 42205184 | tf_op jit(solution)/shard_map/while/body/pallas_call | solution.py:49
  2003.6 29.7 %body.18 = f32[512,2048]{1,0:T(8,128)} custom-call(bf16[512,2048]{1,0:T(8,128)(2,1)} %gather_fusion.2, bf16[2,1,2752,2048]{3,2,1,0:T(8,128)(2,1)} %get-tuple-element.1601.gate_ref, bf16[2,1,2752,2048]{3,2,1,0:T(8,128)(2,1)} %get-tuple-element.1602.up_ref, bf16[2,1,2752,2048]{3,2,1,0:T(8,128)(2,1)} %get-tuple-element.1603.down_ref), custom_call_target="tpu_custom_call" | custom-call | flops 17314086912 | bytes 42205184 | tf_op jit(solution)/shard_map/while/body/pallas_call | solution.py:49
  2083.9 29.7 %body.18 = f32[512,2048]{1,0:T(8,128)} custom-call(bf16[512,2048]{1,0:T(8,128)(2,1)} %gather_fusion.2, bf16[2,1,2752,2048]{3,2,1,0:T(8,128)(2,1)} %get-tuple-element.1601.gate_ref, bf16[2,1,2752,2048]{3,2,1,0:T(8,128)(2,1)} %get-tuple-element.1602.up_ref, bf16[2,1,2752,2048]{3,2,1,0:T(8,128)(2,1)} %get-tuple-element.1603.down_ref), custom_call_target="tpu_custom_call" | custom-call | flops 17314086912 | bytes 42205184 | tf_op jit(solution)/shard_map/while/body/pallas_call | solution.py:49
  2164.1 112.9 %while.95 = (s32[]{:T(128)}, f32[256,2048]{1,0:T(8,128)S(1)}, f32[256,2048]{1,0:T(8,128)}, bf16[256,2048]{1,0:T(8,128)(2,1)S(1)}, bf16[2,256,2048]{2,1,0:T(8,128...) while((s32[]{:T(128)}, f32[256,2048]{1,0:T(8,128)S(1)}, ...), condition=%wide.region_15.16_spmd, body=%wide.region_14.15_spmd.sunk | while | flops 17324574720 | bytes 114569592 | solution.py:218
  2175.1 29.7 %body.19 = f32[512,2048]{1,0:T(8,128)} custom-call(bf16[512,2048]{1,0:T(8,128)(2,1)} %gather_fusion.3, bf16[2,1,2752,2048]{3,2,1,0:T(8,128)(2,1)} %get-tuple-element.1656.gate_ref, bf16[2,1,2752,2048]{3,2,1,0:T(8,128)(2,1)} %get-tuple-element.1657.up_ref, bf16[2,1,2752,2048]{3,2,1,0:T(8,128)(2,1)} %get-tuple-element.1658.down_ref), custom_call_target="tpu_custom_call" | custom-call | flops 17314086912 | bytes 42205184 | tf_op jit(solution)/shard_map/while/body/pallas_call | solution.py:49
  2231.7 29.7 %body.19 = f32[512,2048]{1,0:T(8,128)} custom-call(bf16[512,2048]{1,0:T(8,128)(2,1)} %gather_fusion.3, bf16[2,1,2752,2048]{3,2,1,0:T(8,128)(2,1)} %get-tuple-element.1656.gate_ref, bf16[2,1,2752,2048]{3,2,1,0:T(8,128)(2,1)} %get-tuple-element.1657.up_ref, bf16[2,1,2752,2048]{3,2,1,0:T(8,128)(2,1)} %get-tuple-element.1658.down_ref), custom_call_target="tpu_custom_call" | custom-call | flops 17314086912 | bytes 42205184 | tf_op jit(solution)/shard_map/while/body/pallas_call | solution.py:49
  2341.9 21.4 collective-permute-done.44
  2378.8 24.3 gather_fusion.8
  2403.1 24.4 gather_fusion.9
  2473.6 53.8 %collective-permute-done.49 = bf16[1024,2048]{1,0:T(8,128)(2,1)} collective-permute-done((bf16[1024,2048]{1,0:T(8,128)(2,1)}, bf16[1024,2048]{1,0:T(8,128)(2,1)}, u32[]{:S(2)}, u32[]{:S(2)}) %collective-permute-start.49) | collective-permute-done | bytes 4194336 | tf_op jit(solution)/shard_map/ppermute | solution.py:121
  (858 shorter events, 1292.4 us)
Async XLA Ops:
  10.9 118.3 %collective-permute-start.18 = (bf16[2048,2048]{1,0:T(8,128)(2,1)}, bf16[2048,2048]{1,0:T(8,128)(2,1)}, u32[]{:S(2)}, u32[]{:S(2)}) collective-permute-start(bf16[2048,2048]{1,0:T(8,128)(2,1)} %param.17), channel_id=1, source_target_pairs={{0,1},{1,0},{2,3},{3,2},{4,5},{5,4},{6,7},{7,6}} | collective-permute-start | bytes 25165832 | tf_op jit(solution)/shard_map/ppermute | solution.py:127
  14.6 83.4 %collective-permute-start.19 = (bf16[688,2048]{1,0:T(8,128)(2,1)}, bf16[688,2048]{1,0:T(8,128)(2,1)}, u32[]{:S(2)}, u32[]{:S(2)}) collective-permute-start(bf16[688,2048]{1,0:T(8,128)(2,1)} %dynamic-slice_bitcast_fusion.6), channel_id=1, source_target_pairs={{0,2},{1,3},{2,0},{3,1},{4,6},{5,7},{6,4},{7,5}} | collective-permute-start | bytes 8454152 | tf_op jit(solution)/shard_map/ppermute | solution.py:124
  19.1 147.4 %collective-permute-start.21 = (bf16[672,2048]{1,0:T(8,128)(2,1)}, bf16[672,2048]{1,0:T(8,128)(2,1)}, u32[]{:S(2)}, u32[]{:S(2)}) collective-permute-start(bf16[672,2048]{1,0:T(8,128)(2,1)} %pad_maximum_fusion.6), channel_id=1, source_target_pairs={{0,2},{1,3},{2,0},{3,1},{4,6},{5,7},{6,4},{7,5}} | collective-permute-start | bytes 8257544 | tf_op jit(solution)/shard_map/ppermute | solution.py:124
  42.5 163.7 %collective-permute-start.23 = (bf16[1376,2048]{1,0:T(8,128)(2,1)}, bf16[1376,2048]{1,0:T(8,128)(2,1)}, u32[]{:S(2)}, u32[]{:S(2)}) collective-permute-start(bf16[1376,2048]{1,0:T(8,128)(2,1)} %dynamic-slice_bitcast_fusion.5), channel_id=1, source_target_pairs={{0,1},{1,0},{2,3},{3,2},{4,5},{5,4},{6,7},{7,6}} | collective-permute-start | bytes 16908296 | tf_op jit(solution)/shard_map/ppermute | solution.py:127
  98.0 63.7 %collective-permute-start.20 = (bf16[688,2048]{1,0:T(8,128)(2,1)}, bf16[688,2048]{1,0:T(8,128)(2,1)S(1)}, u32[]{:S(2)}, u32[]{:S(2)}) collective-permute-start(bf16[688,2048]{1,0:T(8,128)(2,1)} %collective-permute-done.19), channel_id=1, source_target_pairs={{0,4},{4,0},{1,5},{5,1},{2,6},{6,2},{3,7},{7,3}} | collective-permute-start | bytes 8454152 | tf_op jit(solution)/shard_map/ppermute | solution.py:121
  128.9 86.0 %collective-permute-start.25 = (bf16[1376,2048]{1,0:T(8,128)(2,1)}, bf16[1376,2048]{1,0:T(8,128)(2,1)}, u32[]{:S(2)}, u32[]{:S(2)}) collective-permute-start(bf16[1376,2048]{1,0:T(8,128)(2,1)} %dynamic-slice_bitcast_fusion.3), channel_id=1, source_target_pairs={{0,1},{1,0},{2,3},{3,2},{4,5},{5,4},{6,7},{7,6}} | collective-permute-start | bytes 16908296 | tf_op jit(solution)/shard_map/ppermute | solution.py:127
  137.5 85.6 %collective-permute-start.24 = (bf16[1376,2048]{1,0:T(8,128)(2,1)}, bf16[1376,2048]{1,0:T(8,128)(2,1)}, u32[]{:S(2)}, u32[]{:S(2)}) collective-permute-start(bf16[1376,2048]{1,0:T(8,128)(2,1)} %dynamic-slice_bitcast_fusion.4), channel_id=1, source_target_pairs={{0,1},{1,0},{2,3},{3,2},{4,5},{5,4},{6,7},{7,6}} | collective-permute-start | bytes 16908296 | tf_op jit(solution)/shard_map/ppermute | solution.py:127
  321.2 67.9 %collective-permute-start = (f32[256,2048]{1,0:T(8,128)}, f32[256,2048]{1,0:T(8,128)}, u32[]{:S(2)}, u32[]{:S(2)}) collective-permute-start(f32[256,2048]{1,0:T(8,128)} %get-tuple-element.1439), channel_id=1, source_target_pairs={{0,4},{4,0},{1,5},{5,1},{2,6},{6,2},{3,7},{7,3}} | collective-permute-start | bytes 6291464 | tf_op jit(solution)/shard_map/while/body/ppermute | solution.py:121
  322.8 63.6 %collective-permute-start.1 = (bf16[256,2048]{1,0:T(8,128)(2,1)S(1)}, bf16[256,2048]{1,0:T(8,128)(2,1)}, u32[]{:S(2)}, u32[]{:S(2)}) collective-permute-start(bf16[256,2048]{1,0:T(8,128)(2,1)S(1)} %get-tuple-element.1440), channel_id=1, source_target_pairs={{0,2},{1,3},{2,0},{3,1},{4,6},{5,7},{6,4},{7,5}} | collective-permute-start | bytes 3145736 | tf_op jit(solution)/shard_map/while/body/ppermute | solution.py:124
  404.8 66.7 %collective-permute-start = (f32[256,2048]{1,0:T(8,128)}, f32[256,2048]{1,0:T(8,128)}, u32[]{:S(2)}, u32[]{:S(2)}) collective-permute-start(f32[256,2048]{1,0:T(8,128)} %get-tuple-element.1439), channel_id=1, source_target_pairs={{0,4},{4,0},{1,5},{5,1},{2,6},{6,2},{3,7},{7,3}} | collective-permute-start | bytes 6291464 | tf_op jit(solution)/shard_map/while/body/ppermute | solution.py:121
  406.3 62.4 %collective-permute-start.1 = (bf16[256,2048]{1,0:T(8,128)(2,1)S(1)}, bf16[256,2048]{1,0:T(8,128)(2,1)}, u32[]{:S(2)}, u32[]{:S(2)}) collective-permute-start(bf16[256,2048]{1,0:T(8,128)(2,1)S(1)} %get-tuple-element.1440), channel_id=1, source_target_pairs={{0,2},{1,3},{2,0},{3,1},{4,6},{5,7},{6,4},{7,5}} | collective-permute-start | bytes 3145736 | tf_op jit(solution)/shard_map/while/body/ppermute | solution.py:124
  487.7 65.9 %collective-permute-start = (f32[256,2048]{1,0:T(8,128)}, f32[256,2048]{1,0:T(8,128)}, u32[]{:S(2)}, u32[]{:S(2)}) collective-permute-start(f32[256,2048]{1,0:T(8,128)} %get-tuple-element.1439), channel_id=1, source_target_pairs={{0,4},{4,0},{1,5},{5,1},{2,6},{6,2},{3,7},{7,3}} | collective-permute-start | bytes 6291464 | tf_op jit(solution)/shard_map/while/body/ppermute | solution.py:121
  489.3 61.6 %collective-permute-start.1 = (bf16[256,2048]{1,0:T(8,128)(2,1)S(1)}, bf16[256,2048]{1,0:T(8,128)(2,1)}, u32[]{:S(2)}, u32[]{:S(2)}) collective-permute-start(bf16[256,2048]{1,0:T(8,128)(2,1)S(1)} %get-tuple-element.1440), channel_id=1, source_target_pairs={{0,2},{1,3},{2,0},{3,1},{4,6},{5,7},{6,4},{7,5}} | collective-permute-start | bytes 3145736 | tf_op jit(solution)/shard_map/while/body/ppermute | solution.py:124
  569.9 65.0 %collective-permute-start = (f32[256,2048]{1,0:T(8,128)}, f32[256,2048]{1,0:T(8,128)}, u32[]{:S(2)}, u32[]{:S(2)}) collective-permute-start(f32[256,2048]{1,0:T(8,128)} %get-tuple-element.1439), channel_id=1, source_target_pairs={{0,4},{4,0},{1,5},{5,1},{2,6},{6,2},{3,7},{7,3}} | collective-permute-start | bytes 6291464 | tf_op jit(solution)/shard_map/while/body/ppermute | solution.py:121
  571.4 60.7 %collective-permute-start.1 = (bf16[256,2048]{1,0:T(8,128)(2,1)S(1)}, bf16[256,2048]{1,0:T(8,128)(2,1)}, u32[]{:S(2)}, u32[]{:S(2)}) collective-permute-start(bf16[256,2048]{1,0:T(8,128)(2,1)S(1)} %get-tuple-element.1440), channel_id=1, source_target_pairs={{0,2},{1,3},{2,0},{3,1},{4,6},{5,7},{6,4},{7,5}} | collective-permute-start | bytes 3145736 | tf_op jit(solution)/shard_map/while/body/ppermute | solution.py:124
  651.1 64.2 %collective-permute-start = (f32[256,2048]{1,0:T(8,128)}, f32[256,2048]{1,0:T(8,128)}, u32[]{:S(2)}, u32[]{:S(2)}) collective-permute-start(f32[256,2048]{1,0:T(8,128)} %get-tuple-element.1439), channel_id=1, source_target_pairs={{0,4},{4,0},{1,5},{5,1},{2,6},{6,2},{3,7},{7,3}} | collective-permute-start | bytes 6291464 | tf_op jit(solution)/shard_map/while/body/ppermute | solution.py:121
  652.6 59.9 %collective-permute-start.1 = (bf16[256,2048]{1,0:T(8,128)(2,1)S(1)}, bf16[256,2048]{1,0:T(8,128)(2,1)}, u32[]{:S(2)}, u32[]{:S(2)}) collective-permute-start(bf16[256,2048]{1,0:T(8,128)(2,1)S(1)} %get-tuple-element.1440), channel_id=1, source_target_pairs={{0,2},{1,3},{2,0},{3,1},{4,6},{5,7},{6,4},{7,5}} | collective-permute-start | bytes 3145736 | tf_op jit(solution)/shard_map/while/body/ppermute | solution.py:124
  731.6 63.3 %collective-permute-start = (f32[256,2048]{1,0:T(8,128)}, f32[256,2048]{1,0:T(8,128)}, u32[]{:S(2)}, u32[]{:S(2)}) collective-permute-start(f32[256,2048]{1,0:T(8,128)} %get-tuple-element.1439), channel_id=1, source_target_pairs={{0,4},{4,0},{1,5},{5,1},{2,6},{6,2},{3,7},{7,3}} | collective-permute-start | bytes 6291464 | tf_op jit(solution)/shard_map/while/body/ppermute | solution.py:121
  733.1 59.0 %collective-permute-start.1 = (bf16[256,2048]{1,0:T(8,128)(2,1)S(1)}, bf16[256,2048]{1,0:T(8,128)(2,1)}, u32[]{:S(2)}, u32[]{:S(2)}) collective-permute-start(bf16[256,2048]{1,0:T(8,128)(2,1)S(1)} %get-tuple-element.1440), channel_id=1, source_target_pairs={{0,2},{1,3},{2,0},{3,1},{4,6},{5,7},{6,4},{7,5}} | collective-permute-start | bytes 3145736 | tf_op jit(solution)/shard_map/while/body/ppermute | solution.py:124
  811.1 62.4 %collective-permute-start = (f32[256,2048]{1,0:T(8,128)}, f32[256,2048]{1,0:T(8,128)}, u32[]{:S(2)}, u32[]{:S(2)}) collective-permute-start(f32[256,2048]{1,0:T(8,128)} %get-tuple-element.1439), channel_id=1, source_target_pairs={{0,4},{4,0},{1,5},{5,1},{2,6},{6,2},{3,7},{7,3}} | collective-permute-start | bytes 6291464 | tf_op jit(solution)/shard_map/while/body/ppermute | solution.py:121
  812.6 58.1 %collective-permute-start.1 = (bf16[256,2048]{1,0:T(8,128)(2,1)S(1)}, bf16[256,2048]{1,0:T(8,128)(2,1)}, u32[]{:S(2)}, u32[]{:S(2)}) collective-permute-start(bf16[256,2048]{1,0:T(8,128)(2,1)S(1)} %get-tuple-element.1440), channel_id=1, source_target_pairs={{0,2},{1,3},{2,0},{3,1},{4,6},{5,7},{6,4},{7,5}} | collective-permute-start | bytes 3145736 | tf_op jit(solution)/shard_map/while/body/ppermute | solution.py:124
  889.8 61.6 %collective-permute-start = (f32[256,2048]{1,0:T(8,128)}, f32[256,2048]{1,0:T(8,128)}, u32[]{:S(2)}, u32[]{:S(2)}) collective-permute-start(f32[256,2048]{1,0:T(8,128)} %get-tuple-element.1439), channel_id=1, source_target_pairs={{0,4},{4,0},{1,5},{5,1},{2,6},{6,2},{3,7},{7,3}} | collective-permute-start | bytes 6291464 | tf_op jit(solution)/shard_map/while/body/ppermute | solution.py:121
  891.3 57.3 %collective-permute-start.1 = (bf16[256,2048]{1,0:T(8,128)(2,1)S(1)}, bf16[256,2048]{1,0:T(8,128)(2,1)}, u32[]{:S(2)}, u32[]{:S(2)}) collective-permute-start(bf16[256,2048]{1,0:T(8,128)(2,1)S(1)} %get-tuple-element.1440), channel_id=1, source_target_pairs={{0,2},{1,3},{2,0},{3,1},{4,6},{5,7},{6,4},{7,5}} | collective-permute-start | bytes 3145736 | tf_op jit(solution)/shard_map/while/body/ppermute | solution.py:124
  1216.1 93.0 %collective-permute-start.32 = (bf16[1024,2048]{1,0:T(8,128)(2,1)S(1)}, bf16[1024,2048]{1,0:T(8,128)(2,1)S(1)}, u32[]{:S(2)}, u32[]{:S(2)}) collective-permute-start(bf16[1024,2048]{1,0:T(8,128)(2,1)S(1)} %get-tuple-element.937), channel_id=1, source_target_pairs={{0,2},{1,3},{2,0},{3,1},{4,6},{5,7},{6,4},{7,5}} | collective-permute-start | bytes 12582920 | tf_op jit(solution)/shard_map/ppermute | solution.py:124
  1216.3 94.6 %collective-permute-start.33 = (bf16[1024,2048]{1,0:T(8,128)(2,1)S(1)}, bf16[1024,2048]{1,0:T(8,128)(2,1)S(1)}, u32[]{:S(2)}, u32[]{:S(2)}) collective-permute-start(bf16[1024,2048]{1,0:T(8,128)(2,1)S(1)} %get-tuple-element.937), channel_id=1, source_target_pairs={{0,4},{4,0},{1,5},{5,1},{2,6},{6,2},{3,7},{7,3}} | collective-permute-start | bytes 12582920 | tf_op jit(solution)/shard_map/ppermute | solution.py:121
  1363.0 62.9 %collective-permute-start.36 = (bf16[4096,2048]{1,0:T(8,128)(2,1)}, bf16[4096,2048]{1,0:T(8,128)(2,1)}, u32[]{:S(2)}, u32[]{:S(2)}) collective-permute-start(bf16[4096,2048]{1,0:T(8,128)(2,1)} %get-tuple-element.983), channel_id=1, source_target_pairs={{0,1},{1,0},{2,3},{3,2},{4,5},{5,4},{6,7},{7,6}} | collective-permute-start | bytes 50331656 | tf_op jit(solution)/shard_map/ppermute | solution.py:127
  1500.2 66.7 %collective-permute-start.9 = (f32[256,2048]{1,0:T(8,128)}, f32[256,2048]{1,0:T(8,128)}, u32[]{:S(2)}, u32[]{:S(2)}) collective-permute-start(f32[256,2048]{1,0:T(8,128)} %get-tuple-element.1565), channel_id=1, source_target_pairs={{0,4},{4,0},{1,5},{5,1},{2,6},{6,2},{3,7},{7,3}} | collective-permute-start | bytes 6291464 | tf_op jit(solution)/shard_map/while/body/ppermute | solution.py:121
  1500.8 63.3 %collective-permute-start.10 = (bf16[256,2048]{1,0:T(8,128)(2,1)S(1)}, bf16[256,2048]{1,0:T(8,128)(2,1)}, u32[]{:S(2)}, u32[]{:S(2)}) collective-permute-start(bf16[256,2048]{1,0:T(8,128)(2,1)S(1)} %get-tuple-element.1566), channel_id=1, source_target_pairs={{0,2},{1,3},{2,0},{3,1},{4,6},{5,7},{6,4},{7,5}} | collective-permute-start | bytes 3145736 | tf_op jit(solution)/shard_map/while/body/ppermute | solution.py:124
  1581.7 67.9 %collective-permute-start.9 = (f32[256,2048]{1,0:T(8,128)}, f32[256,2048]{1,0:T(8,128)}, u32[]{:S(2)}, u32[]{:S(2)}) collective-permute-start(f32[256,2048]{1,0:T(8,128)} %get-tuple-element.1565), channel_id=1, source_target_pairs={{0,4},{4,0},{1,5},{5,1},{2,6},{6,2},{3,7},{7,3}} | collective-permute-start | bytes 6291464 | tf_op jit(solution)/shard_map/while/body/ppermute | solution.py:121
  1582.4 64.5 %collective-permute-start.10 = (bf16[256,2048]{1,0:T(8,128)(2,1)S(1)}, bf16[256,2048]{1,0:T(8,128)(2,1)}, u32[]{:S(2)}, u32[]{:S(2)}) collective-permute-start(bf16[256,2048]{1,0:T(8,128)(2,1)S(1)} %get-tuple-element.1566), channel_id=1, source_target_pairs={{0,2},{1,3},{2,0},{3,1},{4,6},{5,7},{6,4},{7,5}} | collective-permute-start | bytes 3145736 | tf_op jit(solution)/shard_map/while/body/ppermute | solution.py:124
  1664.5 68.9 %collective-permute-start.9 = (f32[256,2048]{1,0:T(8,128)}, f32[256,2048]{1,0:T(8,128)}, u32[]{:S(2)}, u32[]{:S(2)}) collective-permute-start(f32[256,2048]{1,0:T(8,128)} %get-tuple-element.1565), channel_id=1, source_target_pairs={{0,4},{4,0},{1,5},{5,1},{2,6},{6,2},{3,7},{7,3}} | collective-permute-start | bytes 6291464 | tf_op jit(solution)/shard_map/while/body/ppermute | solution.py:121
  1665.1 65.5 %collective-permute-start.10 = (bf16[256,2048]{1,0:T(8,128)(2,1)S(1)}, bf16[256,2048]{1,0:T(8,128)(2,1)}, u32[]{:S(2)}, u32[]{:S(2)}) collective-permute-start(bf16[256,2048]{1,0:T(8,128)(2,1)S(1)} %get-tuple-element.1566), channel_id=1, source_target_pairs={{0,2},{1,3},{2,0},{3,1},{4,6},{5,7},{6,4},{7,5}} | collective-permute-start | bytes 3145736 | tf_op jit(solution)/shard_map/while/body/ppermute | solution.py:124
  1748.3 68.1 %collective-permute-start.9 = (f32[256,2048]{1,0:T(8,128)}, f32[256,2048]{1,0:T(8,128)}, u32[]{:S(2)}, u32[]{:S(2)}) collective-permute-start(f32[256,2048]{1,0:T(8,128)} %get-tuple-element.1565), channel_id=1, source_target_pairs={{0,4},{4,0},{1,5},{5,1},{2,6},{6,2},{3,7},{7,3}} | collective-permute-start | bytes 6291464 | tf_op jit(solution)/shard_map/while/body/ppermute | solution.py:121
  1748.9 64.7 %collective-permute-start.10 = (bf16[256,2048]{1,0:T(8,128)(2,1)S(1)}, bf16[256,2048]{1,0:T(8,128)(2,1)}, u32[]{:S(2)}, u32[]{:S(2)}) collective-permute-start(bf16[256,2048]{1,0:T(8,128)(2,1)S(1)} %get-tuple-element.1566), channel_id=1, source_target_pairs={{0,2},{1,3},{2,0},{3,1},{4,6},{5,7},{6,4},{7,5}} | collective-permute-start | bytes 3145736 | tf_op jit(solution)/shard_map/while/body/ppermute | solution.py:124
  1831.2 67.2 %collective-permute-start.9 = (f32[256,2048]{1,0:T(8,128)}, f32[256,2048]{1,0:T(8,128)}, u32[]{:S(2)}, u32[]{:S(2)}) collective-permute-start(f32[256,2048]{1,0:T(8,128)} %get-tuple-element.1565), channel_id=1, source_target_pairs={{0,4},{4,0},{1,5},{5,1},{2,6},{6,2},{3,7},{7,3}} | collective-permute-start | bytes 6291464 | tf_op jit(solution)/shard_map/while/body/ppermute | solution.py:121
  1831.8 63.8 %collective-permute-start.10 = (bf16[256,2048]{1,0:T(8,128)(2,1)S(1)}, bf16[256,2048]{1,0:T(8,128)(2,1)}, u32[]{:S(2)}, u32[]{:S(2)}) collective-permute-start(bf16[256,2048]{1,0:T(8,128)(2,1)S(1)} %get-tuple-element.1566), channel_id=1, source_target_pairs={{0,2},{1,3},{2,0},{3,1},{4,6},{5,7},{6,4},{7,5}} | collective-permute-start | bytes 3145736 | tf_op jit(solution)/shard_map/while/body/ppermute | solution.py:124
  1913.3 66.4 %collective-permute-start.9 = (f32[256,2048]{1,0:T(8,128)}, f32[256,2048]{1,0:T(8,128)}, u32[]{:S(2)}, u32[]{:S(2)}) collective-permute-start(f32[256,2048]{1,0:T(8,128)} %get-tuple-element.1565), channel_id=1, source_target_pairs={{0,4},{4,0},{1,5},{5,1},{2,6},{6,2},{3,7},{7,3}} | collective-permute-start | bytes 6291464 | tf_op jit(solution)/shard_map/while/body/ppermute | solution.py:121
  1914.0 62.9 %collective-permute-start.10 = (bf16[256,2048]{1,0:T(8,128)(2,1)S(1)}, bf16[256,2048]{1,0:T(8,128)(2,1)}, u32[]{:S(2)}, u32[]{:S(2)}) collective-permute-start(bf16[256,2048]{1,0:T(8,128)(2,1)S(1)} %get-tuple-element.1566), channel_id=1, source_target_pairs={{0,2},{1,3},{2,0},{3,1},{4,6},{5,7},{6,4},{7,5}} | collective-permute-start | bytes 3145736 | tf_op jit(solution)/shard_map/while/body/ppermute | solution.py:124
  1994.5 65.5 %collective-permute-start.9 = (f32[256,2048]{1,0:T(8,128)}, f32[256,2048]{1,0:T(8,128)}, u32[]{:S(2)}, u32[]{:S(2)}) collective-permute-start(f32[256,2048]{1,0:T(8,128)} %get-tuple-element.1565), channel_id=1, source_target_pairs={{0,4},{4,0},{1,5},{5,1},{2,6},{6,2},{3,7},{7,3}} | collective-permute-start | bytes 6291464 | tf_op jit(solution)/shard_map/while/body/ppermute | solution.py:121
  1995.2 62.1 %collective-permute-start.10 = (bf16[256,2048]{1,0:T(8,128)(2,1)S(1)}, bf16[256,2048]{1,0:T(8,128)(2,1)}, u32[]{:S(2)}, u32[]{:S(2)}) collective-permute-start(bf16[256,2048]{1,0:T(8,128)(2,1)S(1)} %get-tuple-element.1566), channel_id=1, source_target_pairs={{0,2},{1,3},{2,0},{3,1},{4,6},{5,7},{6,4},{7,5}} | collective-permute-start | bytes 3145736 | tf_op jit(solution)/shard_map/while/body/ppermute | solution.py:124
  2074.8 64.7 %collective-permute-start.9 = (f32[256,2048]{1,0:T(8,128)}, f32[256,2048]{1,0:T(8,128)}, u32[]{:S(2)}, u32[]{:S(2)}) collective-permute-start(f32[256,2048]{1,0:T(8,128)} %get-tuple-element.1565), channel_id=1, source_target_pairs={{0,4},{4,0},{1,5},{5,1},{2,6},{6,2},{3,7},{7,3}} | collective-permute-start | bytes 6291464 | tf_op jit(solution)/shard_map/while/body/ppermute | solution.py:121
  2075.5 61.2 %collective-permute-start.10 = (bf16[256,2048]{1,0:T(8,128)(2,1)S(1)}, bf16[256,2048]{1,0:T(8,128)(2,1)}, u32[]{:S(2)}, u32[]{:S(2)}) collective-permute-start(bf16[256,2048]{1,0:T(8,128)(2,1)S(1)} %get-tuple-element.1566), channel_id=1, source_target_pairs={{0,2},{1,3},{2,0},{3,1},{4,6},{5,7},{6,4},{7,5}} | collective-permute-start | bytes 3145736 | tf_op jit(solution)/shard_map/while/body/ppermute | solution.py:124
  2146.2 132.8 %collective-permute-start.46 = (bf16[1376,2048]{1,0:T(8,128)(2,1)}, bf16[1376,2048]{1,0:T(8,128)(2,1)}, u32[]{:S(2)}, u32[]{:S(2)}) collective-permute-start(bf16[1376,2048]{1,0:T(8,128)(2,1)} %get-tuple-element.970), channel_id=1, source_target_pairs={{0,1},{1,0},{2,3},{3,2},{4,5},{5,4},{6,7},{7,6}} | collective-permute-start | bytes 16908296 | tf_op jit(solution)/shard_map/ppermute | solution.py:127
  2156.8 134.4 %collective-permute-start.47 = (bf16[1376,2048]{1,0:T(8,128)(2,1)}, bf16[1376,2048]{1,0:T(8,128)(2,1)}, u32[]{:S(2)}, u32[]{:S(2)}) collective-permute-start(bf16[1376,2048]{1,0:T(8,128)(2,1)} %get-tuple-element.968), channel_id=1, source_target_pairs={{0,1},{1,0},{2,3},{3,2},{4,5},{5,4},{6,7},{7,6}} | collective-permute-start | bytes 16908296 | tf_op jit(solution)/shard_map/ppermute | solution.py:127
  2326.4 110.7 %collective-permute-start.52 = (bf16[1376,2048]{1,0:T(8,128)(2,1)}, bf16[1376,2048]{1,0:T(8,128)(2,1)}, u32[]{:S(2)}, u32[]{:S(2)}) collective-permute-start(bf16[1376,2048]{1,0:T(8,128)(2,1)} %get-tuple-element.960), channel_id=1, source_target_pairs={{0,1},{1,0},{2,3},{3,2},{4,5},{5,4},{6,7},{7,6}} | collective-permute-start | bytes 16908296 | tf_op jit(solution)/shard_map/ppermute | solution.py:127
  2339.8 109.4 %collective-permute-start.51 = (bf16[1376,2048]{1,0:T(8,128)(2,1)}, bf16[1376,2048]{1,0:T(8,128)(2,1)}, u32[]{:S(2)}, u32[]{:S(2)}) collective-permute-start(bf16[1376,2048]{1,0:T(8,128)(2,1)} %get-tuple-element.962), channel_id=1, source_target_pairs={{0,1},{1,0},{2,3},{3,2},{4,5},{5,4},{6,7},{7,6}} | collective-permute-start | bytes 16908296 | tf_op jit(solution)/shard_map/ppermute | solution.py:127
  2368.3 93.2 %collective-permute-start.50 = (bf16[1376,2048]{1,0:T(8,128)(2,1)}, bf16[1376,2048]{1,0:T(8,128)(2,1)}, u32[]{:S(2)}, u32[]{:S(2)}) collective-permute-start(bf16[1376,2048]{1,0:T(8,128)(2,1)} %get-tuple-element.964), channel_id=1, source_target_pairs={{0,1},{1,0},{2,3},{3,2},{4,5},{5,4},{6,7},{7,6}} | collective-permute-start | bytes 16908296 | tf_op jit(solution)/shard_map/ppermute | solution.py:127
  2434.5 92.9 %collective-permute-start.49 = (bf16[1024,2048]{1,0:T(8,128)(2,1)}, bf16[1024,2048]{1,0:T(8,128)(2,1)}, u32[]{:S(2)}, u32[]{:S(2)}) collective-permute-start(bf16[1024,2048]{1,0:T(8,128)(2,1)} %add_convert_fusion.4), channel_id=1, source_target_pairs={{0,4},{4,0},{1,5},{5,1},{2,6},{6,2},{3,7},{7,3}} | collective-permute-start | bytes 12582920 | tf_op jit(solution)/shard_map/ppermute | solution.py:121
  (183 other events, 5941.2 us)

commit v2 on v1

--- a/solution.py
+++ b/solution.py
@@ -10,6 +10,7 @@
 WEIGHT_CHUNKS = 8
 FFN_TILES = 4
 INSTALL_TILES = 4
+COMBINE_ROWS = 512
 
 
 def running_count(mask):
@@ -192,7 +193,8 @@
                 crossed = over_core(pair)
                 new_keep, new_send = compute(i)
                 buffer = put(buffer, i - 3, pair, crossed)
-                return new_keep, new_send, (keep + recv).astype(jnp.bfloat16), jnp.stack([rounded, across]), buffer
+                total = (keep + recv).astype(jnp.bfloat16)
+                return new_keep, new_send, total, jnp.stack([rounded, across]), buffer
 
             def plain(i, carry):
                 return stages(i, carry)
@@ -236,11 +238,13 @@
             place = (relative % 2) * 2 + relative // 2
             flat = ((pos // HALF_CHUNK) * 4 + place) * HALF_CHUNK + pos % HALF_CHUNK
             table = buffer.reshape(max_chunks * 4 * HALF_CHUNK, width)
-            mixture = jnp.zeros((half, width), jnp.float32)
-            for j in range(2):
-                picked = table.at[flat[:, j]].get(mode='promise_in_bounds')
-                mixture = mixture + my_gates[:, j:j + 1] * picked.astype(jnp.float32)
-            hidden_next = (hidden_half.astype(jnp.float32) + mixture).astype(jnp.bfloat16)
+            blocks = []
+            for start in range(0, half, COMBINE_ROWS):
+                part = slice(start, start + COMBINE_ROWS)
+                first_rows, second_rows = [table.at[flat[part, j]].get(mode='promise_in_bounds').astype(jnp.float32) for j in range(2)]
+                mixture = my_gates[part, 0:1] * first_rows + my_gates[part, 1:2] * second_rows
+                blocks.append((hidden_half[part].astype(jnp.float32) + mixture).astype(jnp.bfloat16))
+            hidden_next = jnp.concatenate(blocks, axis=0)
 
             back = [over_core(jnp.where(in_chip, o, inc)) for o, inc in zip(own_part, incoming)]
             first = [jnp.where(in_chip, f, inc) for f, inc in zip(from_core, incoming)]

time: 2560 us -> 2530 us (0.988)
  local copies, waits for them, and re-layouts: 761 us -> 733 us
    gather x4 -> x8, local copies, waits for them, and re-layouts: 97.4 us -> 53 us  [layer_fn(): table.at[flat[part, j]].get(mode='promise_in_bounds').astype(jnp.float32)]
  transfers between devices with their start and end apart: 143 -> 143, of which waited for: 30 -> 30; matrix products, arithmetic and copies ran while one was open for 34% -> 34% of each run, Pallas kernels for 26% -> 27%
where the time goes in v2:
time: 2530 us; the launch traced here: 2510 us
  local copies, waits for them, and re-layouts  733 us (29%)
  Pallas kernels  725 us (29%)
  waiting for transfers between devices  560 us (22%)
  other arithmetic  365 us (14%)
  starting transfers between devices  104 us (4%)
    pallas_call x22, Pallas kernels, expert_mlp(): pl.pallas_call(mlp_kernel, grid=(FFN_TILES,), in_specs=[row_block, weight...  651 us
    ppermute x76, waiting for transfers between devices, over_x(): return lax.ppermute(arr, 'ep', [(i, i ^ 2) for i in range(group_size)])  369 us
    ppermute x26, waiting for transfers between devices, over_tp(): return lax.ppermute(arr, 'tp', [(0, 1), (1, 0)])  170 us
    gather x22, local copies, waits for them, and re-layouts, compute(): rows = rows_all.at[idx].get(mode='promise_in_bounds')  147 us
    dynamic_update_slice x48, local copies, waits for them, and re-layouts, with_swap(): landed.append(lax.dynamic_update_slice(inc, piece, (start, 0, 0)))  101 us
    dynamic_slice x48, local copies, waits for them, and re-layouts, with_swap(): piece = over_x(lax.dynamic_slice(out, (start, 0, 0), (step, 8, width)))  99.1 us
    another operation x30, local copies, waits for them, and re-layouts  85.7 us
    dynamic_update_slice x26, other arithmetic, put(): return lax.dynamic_update_slice(buffer, block, (jnp.maximum(i, 0), 0, 0, 0))  82.1 us
  transfers between devices with their start and end apart: 143, of which 30 were waited for; matrix products, arithmetic and copies ran while one was open for 34% of the time, Pallas kernels for 27%

profile of v2, /device:TPU:0, one launch (start us, length us, event | category | flops | bytes accessed | tf_op | source)
XLA Modules:
  0.0 2510.6 jit_solution(13960821178854966799)
XLA Ops:
  20.4 16.0 fusion.96
  57.8 18.7 fusion.97
  108.5 20.0 convert_reduce_fusion
  137.3 24.0 collective-permute-done.20
  176.1 20.2 convert_reduce_fusion.1
  246.0 29.5 %shard_map.111 = f32[512,2048]{1,0:T(8,128)} custom-call(bf16[512,2048]{1,0:T(8,128)(2,1)} %gather_fusion.4, bf16[2,1,2752,2048]{3,2,1,0:T(8,128)(2,1)} %bitcast.348, bf16[2,1,2752,2048]{3,2,1,0:T(8,128)(2,1)} %bitcast.346, bf16[2,1,2752,2048]{3,2,1,0:T(8,128)(2,1)} %own_ref.3), custom_call_target="tpu_custom_call" | custom-call | flops 17314086912 | bytes 42205184 | tf_op jit(solution)/shard_map/pallas_call | solution.py:50
  279.5 34.0 %broadcast_in_dim.130 = bf16[16,4,256,2048]{3,2,1,0:T(8,128)(2,1)} broadcast(bf16[]{:T(256)} %constant.449.clone.1), dimensions={} | broadcast | bytes 67108864 | tf_op jit(solution)/shard_map/broadcast_in_dim | solution.py:274
  324.6 646.3 %while.92 = (s32[]{:T(128)}, f32[256,2048]{1,0:T(8,128)S(1)}, f32[256,2048]{1,0:T(8,128)}, bf16[256,2048]{1,0:T(8,128)(2,1)S(1)}, bf16[2,256,2048]{2,1,0:T(8,128...) while((s32[]{:T(128)}, f32[256,2048]{1,0:T(8,128)S(1)}, ...), condition=%wide.region_4.5_spmd, body=%wide.region_3.4_spmd.sunk | while | flops 17324574720 | bytes 140260032 | solution.py:219
  343.1 29.6 %body.16 = f32[512,2048]{1,0:T(8,128)} custom-call(bf16[512,2048]{1,0:T(8,128)(2,1)} %gather_fusion, bf16[2,1,2752,2048]{3,2,1,0:T(8,128)(2,1)} %get-tuple-element.1487.gate_ref, bf16[2,1,2752,2048]{3,2,1,0:T(8,128)(2,1)} %get-tuple-element.1488.up_ref, bf16[2,1,2752,2048]{3,2,1,0:T(8,128)(2,1)} %get-tuple-element.1489.down_ref), custom_call_target="tpu_custom_call" | custom-call | flops 17314086912 | bytes 42205184 | tf_op jit(solution)/shard_map/while/body/pallas_call | solution.py:50
  382.2 15.8 collective-permute-done.1
  425.6 29.6 %body.16 = f32[512,2048]{1,0:T(8,128)} custom-call(bf16[512,2048]{1,0:T(8,128)(2,1)} %gather_fusion, bf16[2,1,2752,2048]{3,2,1,0:T(8,128)(2,1)} %get-tuple-element.1487.gate_ref, bf16[2,1,2752,2048]{3,2,1,0:T(8,128)(2,1)} %get-tuple-element.1488.up_ref, bf16[2,1,2752,2048]{3,2,1,0:T(8,128)(2,1)} %get-tuple-element.1489.down_ref), custom_call_target="tpu_custom_call" | custom-call | flops 17314086912 | bytes 42205184 | tf_op jit(solution)/shard_map/while/body/pallas_call | solution.py:50
  464.7 15.9 collective-permute-done.1
  508.2 29.6 %body.16 = f32[512,2048]{1,0:T(8,128)} custom-call(bf16[512,2048]{1,0:T(8,128)(2,1)} %gather_fusion, bf16[2,1,2752,2048]{3,2,1,0:T(8,128)(2,1)} %get-tuple-element.1487.gate_ref, bf16[2,1,2752,2048]{3,2,1,0:T(8,128)(2,1)} %get-tuple-element.1488.up_ref, bf16[2,1,2752,2048]{3,2,1,0:T(8,128)(2,1)} %get-tuple-element.1489.down_ref), custom_call_target="tpu_custom_call" | custom-call | flops 17314086912 | bytes 42205184 | tf_op jit(solution)/shard_map/while/body/pallas_call | solution.py:50
  547.3 15.6 collective-permute-done.1
  590.6 29.6 %body.16 = f32[512,2048]{1,0:T(8,128)} custom-call(bf16[512,2048]{1,0:T(8,128)(2,1)} %gather_fusion, bf16[2,1,2752,2048]{3,2,1,0:T(8,128)(2,1)} %get-tuple-element.1487.gate_ref, bf16[2,1,2752,2048]{3,2,1,0:T(8,128)(2,1)} %get-tuple-element.1488.up_ref, bf16[2,1,2752,2048]{3,2,1,0:T(8,128)(2,1)} %get-tuple-element.1489.down_ref), custom_call_target="tpu_custom_call" | custom-call | flops 17314086912 | bytes 42205184 | tf_op jit(solution)/shard_map/while/body/pallas_call | solution.py:50
  672.0 29.6 %body.16 = f32[512,2048]{1,0:T(8,128)} custom-call(bf16[512,2048]{1,0:T(8,128)(2,1)} %gather_fusion, bf16[2,1,2752,2048]{3,2,1,0:T(8,128)(2,1)} %get-tuple-element.1487.gate_ref, bf16[2,1,2752,2048]{3,2,1,0:T(8,128)(2,1)} %get-tuple-element.1488.up_ref, bf16[2,1,2752,2048]{3,2,1,0:T(8,128)(2,1)} %get-tuple-element.1489.down_ref), custom_call_target="tpu_custom_call" | custom-call | flops 17314086912 | bytes 42205184 | tf_op jit(solution)/shard_map/while/body/pallas_call | solution.py:50
  752.7 29.6 %body.16 = f32[512,2048]{1,0:T(8,128)} custom-call(bf16[512,2048]{1,0:T(8,128)(2,1)} %gather_fusion, bf16[2,1,2752,2048]{3,2,1,0:T(8,128)(2,1)} %get-tuple-element.1487.gate_ref, bf16[2,1,2752,2048]{3,2,1,0:T(8,128)(2,1)} %get-tuple-element.1488.up_ref, bf16[2,1,2752,2048]{3,2,1,0:T(8,128)(2,1)} %get-tuple-element.1489.down_ref), custom_call_target="tpu_custom_call" | custom-call | flops 17314086912 | bytes 42205184 | tf_op jit(solution)/shard_map/while/body/pallas_call | solution.py:50
  832.4 29.6 %body.16 = f32[512,2048]{1,0:T(8,128)} custom-call(bf16[512,2048]{1,0:T(8,128)(2,1)} %gather_fusion, bf16[2,1,2752,2048]{3,2,1,0:T(8,128)(2,1)} %get-tuple-element.1487.gate_ref, bf16[2,1,2752,2048]{3,2,1,0:T(8,128)(2,1)} %get-tuple-element.1488.up_ref, bf16[2,1,2752,2048]{3,2,1,0:T(8,128)(2,1)} %get-tuple-element.1489.down_ref), custom_call_target="tpu_custom_call" | custom-call | flops 17314086912 | bytes 42205184 | tf_op jit(solution)/shard_map/while/body/pallas_call | solution.py:50
  911.3 29.6 %body.16 = f32[512,2048]{1,0:T(8,128)} custom-call(bf16[512,2048]{1,0:T(8,128)(2,1)} %gather_fusion, bf16[2,1,2752,2048]{3,2,1,0:T(8,128)(2,1)} %get-tuple-element.1487.gate_ref, bf16[2,1,2752,2048]{3,2,1,0:T(8,128)(2,1)} %get-tuple-element.1488.up_ref, bf16[2,1,2752,2048]{3,2,1,0:T(8,128)(2,1)} %get-tuple-element.1489.down_ref), custom_call_target="tpu_custom_call" | custom-call | flops 17314086912 | bytes 42205184 | tf_op jit(solution)/shard_map/while/body/pallas_call | solution.py:50
  970.9 110.9 %while.93 = (s32[]{:T(128)}, f32[256,2048]{1,0:T(8,128)S(1)}, f32[256,2048]{1,0:T(8,128)}, bf16[256,2048]{1,0:T(8,128)(2,1)S(1)}, bf16[2,256,2048]{2,1,0:T(8,128...) while((s32[]{:T(128)}, f32[256,2048]{1,0:T(8,128)S(1)}, ...), condition=%wide.region_7.8_spmd, body=%wide.region_6.7_spmd.sunk | while | flops 17324574720 | bytes 114569592 | solution.py:220
  984.1 29.5 %body.17 = f32[512,2048]{1,0:T(8,128)} custom-call(bf16[512,2048]{1,0:T(8,128)(2,1)} %gather_fusion.1, bf16[2,1,2752,2048]{3,2,1,0:T(8,128)(2,1)} %get-tuple-element.1542.gate_ref, bf16[2,1,2752,2048]{3,2,1,0:T(8,128)(2,1)} %get-tuple-element.1543.up_ref, bf16[2,1,2752,2048]{3,2,1,0:T(8,128)(2,1)} %get-tuple-element.1544.down_ref), custom_call_target="tpu_custom_call" | custom-call | flops 17314086912 | bytes 42205184 | tf_op jit(solution)/shard_map/while/body/pallas_call | solution.py:50
  1035.6 29.5 %body.17 = f32[512,2048]{1,0:T(8,128)} custom-call(bf16[512,2048]{1,0:T(8,128)(2,1)} %gather_fusion.1, bf16[2,1,2752,2048]{3,2,1,0:T(8,128)(2,1)} %get-tuple-element.1542.gate_ref, bf16[2,1,2752,2048]{3,2,1,0:T(8,128)(2,1)} %get-tuple-element.1543.up_ref, bf16[2,1,2752,2048]{3,2,1,0:T(8,128)(2,1)} %get-tuple-element.1544.down_ref), custom_call_target="tpu_custom_call" | custom-call | flops 17314086912 | bytes 42205184 | tf_op jit(solution)/shard_map/while/body/pallas_call | solution.py:50
  1082.8 46.1 %collective-permute-done.29 = f32[256,2048]{1,0:T(8,128)S(1)} collective-permute-done((f32[256,2048]{1,0:T(8,128)}, f32[256,2048]{1,0:T(8,128)S(1)}, u32[]{:S(2)}, u32[]{:S(2)}) %collective-permute-start.29) | collective-permute-done | bytes 2097184 | tf_op jit(solution)/shard_map/ppermute | solution.py:122
  1138.8 15.3 collective-permute-done.30
  1206.0 92.2 %collective-permute-done.32 = bf16[1024,2048]{1,0:T(8,128)(2,1)S(1)} collective-permute-done((bf16[1024,2048]{1,0:T(8,128)(2,1)S(1)}, bf16[1024,2048]{1,0:T(8,128)(2,1)S(1)}, u32[]{:S(2)}, u32[]{:S(2)}) %collective-permute-start.32) | collective-permute-done | bytes 4194336 | tf_op jit(solution)/shard_map/ppermute | solution.py:125
  1313.0 32.6 %collective-permute-done.34 = bf16[512,2048]{1,0:T(8,128)(2,1)S(1)} collective-permute-done((bf16[512,2048]{1,0:T(8,128)(2,1)S(1)}, bf16[512,2048]{1,0:T(8,128)(2,1)S(1)}, u32[]{:S(2)}, u32[]{:S(2)}) %collective-permute-start.34) | collective-permute-done | bytes 2097184 | tf_op jit(solution)/shard_map/ppermute | solution.py:122
  1366.4 17.9 collective-permute-done.39
  1434.9 29.6 %shard_map.112 = f32[512,2048]{1,0:T(8,128)} custom-call(bf16[512,2048]{1,0:T(8,128)(2,1)} %gather_fusion.9, bf16[2,1,2752,2048]{3,2,1,0:T(8,128)(2,1)} %get-tuple-element.1684, bf16[2,1,2752,2048]{3,2,1,0:T(8,128)(2,1)} %get-tuple-element.1680, bf16[2,1,2752,2048]{3,2,1,0:T(8,128)(2,1)} %get-tuple-element.1676), custom_call_target="tpu_custom_call" | custom-call | flops 17314086912 | bytes 42205184 | tf_op jit(solution)/shard_map/pallas_call | solution.py:50
  1479.6 656.1 %while.94 = (s32[]{:T(128)}, f32[256,2048]{1,0:T(8,128)S(1)}, f32[256,2048]{1,0:T(8,128)}, bf16[256,2048]{1,0:T(8,128)(2,1)S(1)}, bf16[2,256,2048]{2,1,0:T(8,128...) while((s32[]{:T(128)}, f32[256,2048]{1,0:T(8,128)S(1)}, ...), condition=%wide.region_13.14_spmd, body=%wide.region_12.13_spmd.sunk | while | flops 17324574720 | bytes 140260032 | solution.py:219
  1497.1 29.7 %body.18 = f32[512,2048]{1,0:T(8,128)} custom-call(bf16[512,2048]{1,0:T(8,128)(2,1)} %gather_fusion.2, bf16[2,1,2752,2048]{3,2,1,0:T(8,128)(2,1)} %get-tuple-element.1613.gate_ref, bf16[2,1,2752,2048]{3,2,1,0:T(8,128)(2,1)} %get-tuple-element.1614.up_ref, bf16[2,1,2752,2048]{3,2,1,0:T(8,128)(2,1)} %get-tuple-element.1615.down_ref), custom_call_target="tpu_custom_call" | custom-call | flops 17314086912 | bytes 42205184 | tf_op jit(solution)/shard_map/while/body/pallas_call | solution.py:50
  1578.8 29.7 %body.18 = f32[512,2048]{1,0:T(8,128)} custom-call(bf16[512,2048]{1,0:T(8,128)(2,1)} %gather_fusion.2, bf16[2,1,2752,2048]{3,2,1,0:T(8,128)(2,1)} %get-tuple-element.1613.gate_ref, bf16[2,1,2752,2048]{3,2,1,0:T(8,128)(2,1)} %get-tuple-element.1614.up_ref, bf16[2,1,2752,2048]{3,2,1,0:T(8,128)(2,1)} %get-tuple-element.1615.down_ref), custom_call_target="tpu_custom_call" | custom-call | flops 17314086912 | bytes 42205184 | tf_op jit(solution)/shard_map/while/body/pallas_call | solution.py:50
  1618.7 16.1 collective-permute-done.10
  1661.6 29.7 %body.18 = f32[512,2048]{1,0:T(8,128)} custom-call(bf16[512,2048]{1,0:T(8,128)(2,1)} %gather_fusion.2, bf16[2,1,2752,2048]{3,2,1,0:T(8,128)(2,1)} %get-tuple-element.1613.gate_ref, bf16[2,1,2752,2048]{3,2,1,0:T(8,128)(2,1)} %get-tuple-element.1614.up_ref, bf16[2,1,2752,2048]{3,2,1,0:T(8,128)(2,1)} %get-tuple-element.1615.down_ref), custom_call_target="tpu_custom_call" | custom-call | flops 17314086912 | bytes 42205184 | tf_op jit(solution)/shard_map/while/body/pallas_call | solution.py:50
  1700.7 18.1 collective-permute-done.10
  1745.5 29.7 %body.18 = f32[512,2048]{1,0:T(8,128)} custom-call(bf16[512,2048]{1,0:T(8,128)(2,1)} %gather_fusion.2, bf16[2,1,2752,2048]{3,2,1,0:T(8,128)(2,1)} %get-tuple-element.1613.gate_ref, bf16[2,1,2752,2048]{3,2,1,0:T(8,128)(2,1)} %get-tuple-element.1614.up_ref, bf16[2,1,2752,2048]{3,2,1,0:T(8,128)(2,1)} %get-tuple-element.1615.down_ref), custom_call_target="tpu_custom_call" | custom-call | flops 17314086912 | bytes 42205184 | tf_op jit(solution)/shard_map/while/body/pallas_call | solution.py:50
  1784.7 17.3 collective-permute-done.10
  1828.7 29.7 %body.18 = f32[512,2048]{1,0:T(8,128)} custom-call(bf16[512,2048]{1,0:T(8,128)(2,1)} %gather_fusion.2, bf16[2,1,2752,2048]{3,2,1,0:T(8,128)(2,1)} %get-tuple-element.1613.gate_ref, bf16[2,1,2752,2048]{3,2,1,0:T(8,128)(2,1)} %get-tuple-element.1614.up_ref, bf16[2,1,2752,2048]{3,2,1,0:T(8,128)(2,1)} %get-tuple-element.1615.down_ref), custom_call_target="tpu_custom_call" | custom-call | flops 17314086912 | bytes 42205184 | tf_op jit(solution)/shard_map/while/body/pallas_call | solution.py:50
  1867.9 16.4 collective-permute-done.10
  1911.2 29.7 %body.18 = f32[512,2048]{1,0:T(8,128)} custom-call(bf16[512,2048]{1,0:T(8,128)(2,1)} %gather_fusion.2, bf16[2,1,2752,2048]{3,2,1,0:T(8,128)(2,1)} %get-tuple-element.1613.gate_ref, bf16[2,1,2752,2048]{3,2,1,0:T(8,128)(2,1)} %get-tuple-element.1614.up_ref, bf16[2,1,2752,2048]{3,2,1,0:T(8,128)(2,1)} %get-tuple-element.1615.down_ref), custom_call_target="tpu_custom_call" | custom-call | flops 17314086912 | bytes 42205184 | tf_op jit(solution)/shard_map/while/body/pallas_call | solution.py:50
  1950.3 15.6 collective-permute-done.10
  1992.6 29.7 %body.18 = f32[512,2048]{1,0:T(8,128)} custom-call(bf16[512,2048]{1,0:T(8,128)(2,1)} %gather_fusion.2, bf16[2,1,2752,2048]{3,2,1,0:T(8,128)(2,1)} %get-tuple-element.1613.gate_ref, bf16[2,1,2752,2048]{3,2,1,0:T(8,128)(2,1)} %get-tuple-element.1614.up_ref, bf16[2,1,2752,2048]{3,2,1,0:T(8,128)(2,1)} %get-tuple-element.1615.down_ref), custom_call_target="tpu_custom_call" | custom-call | flops 17314086912 | bytes 42205184 | tf_op jit(solution)/shard_map/while/body/pallas_call | solution.py:50
  2031.7 14.8 collective-permute-done.10
  2073.2 29.7 %body.18 = f32[512,2048]{1,0:T(8,128)} custom-call(bf16[512,2048]{1,0:T(8,128)(2,1)} %gather_fusion.2, bf16[2,1,2752,2048]{3,2,1,0:T(8,128)(2,1)} %get-tuple-element.1613.gate_ref, bf16[2,1,2752,2048]{3,2,1,0:T(8,128)(2,1)} %get-tuple-element.1614.up_ref, bf16[2,1,2752,2048]{3,2,1,0:T(8,128)(2,1)} %get-tuple-element.1615.down_ref), custom_call_target="tpu_custom_call" | custom-call | flops 17314086912 | bytes 42205184 | tf_op jit(solution)/shard_map/while/body/pallas_call | solution.py:50
  2153.6 112.7 %while.95 = (s32[]{:T(128)}, f32[256,2048]{1,0:T(8,128)S(1)}, f32[256,2048]{1,0:T(8,128)}, bf16[256,2048]{1,0:T(8,128)(2,1)S(1)}, bf16[2,256,2048]{2,1,0:T(8,128...) while((s32[]{:T(128)}, f32[256,2048]{1,0:T(8,128)S(1)}, ...), condition=%wide.region_15.16_spmd, body=%wide.region_14.15_spmd.sunk | while | flops 17324574720 | bytes 114569592 | solution.py:220
  2164.4 29.7 %body.19 = f32[512,2048]{1,0:T(8,128)} custom-call(bf16[512,2048]{1,0:T(8,128)(2,1)} %gather_fusion.3, bf16[2,1,2752,2048]{3,2,1,0:T(8,128)(2,1)} %get-tuple-element.1668.gate_ref, bf16[2,1,2752,2048]{3,2,1,0:T(8,128)(2,1)} %get-tuple-element.1669.up_ref, bf16[2,1,2752,2048]{3,2,1,0:T(8,128)(2,1)} %get-tuple-element.1670.down_ref), custom_call_target="tpu_custom_call" | custom-call | flops 17314086912 | bytes 42205184 | tf_op jit(solution)/shard_map/while/body/pallas_call | solution.py:50
  2221.0 29.7 %body.19 = f32[512,2048]{1,0:T(8,128)} custom-call(bf16[512,2048]{1,0:T(8,128)(2,1)} %gather_fusion.3, bf16[2,1,2752,2048]{3,2,1,0:T(8,128)(2,1)} %get-tuple-element.1668.gate_ref, bf16[2,1,2752,2048]{3,2,1,0:T(8,128)(2,1)} %get-tuple-element.1669.up_ref, bf16[2,1,2752,2048]{3,2,1,0:T(8,128)(2,1)} %get-tuple-element.1670.down_ref), custom_call_target="tpu_custom_call" | custom-call | flops 17314086912 | bytes 42205184 | tf_op jit(solution)/shard_map/while/body/pallas_call | solution.py:50
  2331.3 21.4 collective-permute-done.44
  2442.3 53.4 %collective-permute-done.49 = bf16[1024,2048]{1,0:T(8,128)(2,1)} collective-permute-done((bf16[1024,2048]{1,0:T(8,128)(2,1)}, bf16[1024,2048]{1,0:T(8,128)(2,1)}, u32[]{:S(2)}, u32[]{:S(2)}) %collective-permute-start.49) | collective-permute-done | bytes 4194336 | tf_op jit(solution)/shard_map/ppermute | solution.py:122
  (875 shorter events, 1289.2 us)
Async XLA Ops:
  10.9 117.8 %collective-permute-start.18 = (bf16[2048,2048]{1,0:T(8,128)(2,1)}, bf16[2048,2048]{1,0:T(8,128)(2,1)}, u32[]{:S(2)}, u32[]{:S(2)}) collective-permute-start(bf16[2048,2048]{1,0:T(8,128)(2,1)} %param.17), channel_id=1, source_target_pairs={{0,1},{1,0},{2,3},{3,2},{4,5},{5,4},{6,7},{7,6}} | collective-permute-start | bytes 25165832 | tf_op jit(solution)/shard_map/ppermute | solution.py:128
  14.6 83.0 %collective-permute-start.19 = (bf16[688,2048]{1,0:T(8,128)(2,1)}, bf16[688,2048]{1,0:T(8,128)(2,1)}, u32[]{:S(2)}, u32[]{:S(2)}) collective-permute-start(bf16[688,2048]{1,0:T(8,128)(2,1)} %dynamic-slice_bitcast_fusion.6), channel_id=1, source_target_pairs={{0,2},{1,3},{2,0},{3,1},{4,6},{5,7},{6,4},{7,5}} | collective-permute-start | bytes 8454152 | tf_op jit(solution)/shard_map/ppermute | solution.py:125
  19.1 147.0 %collective-permute-start.21 = (bf16[672,2048]{1,0:T(8,128)(2,1)}, bf16[672,2048]{1,0:T(8,128)(2,1)}, u32[]{:S(2)}, u32[]{:S(2)}) collective-permute-start(bf16[672,2048]{1,0:T(8,128)(2,1)} %pad_maximum_fusion.8), channel_id=1, source_target_pairs={{0,2},{1,3},{2,0},{3,1},{4,6},{5,7},{6,4},{7,5}} | collective-permute-start | bytes 8257544 | tf_op jit(solution)/shard_map/ppermute | solution.py:125
  42.3 163.0 %collective-permute-start.25 = (bf16[1376,2048]{1,0:T(8,128)(2,1)}, bf16[1376,2048]{1,0:T(8,128)(2,1)}, u32[]{:S(2)}, u32[]{:S(2)}) collective-permute-start(bf16[1376,2048]{1,0:T(8,128)(2,1)} %dynamic-slice_bitcast_fusion.3), channel_id=1, source_target_pairs={{0,1},{1,0},{2,3},{3,2},{4,5},{5,4},{6,7},{7,6}} | collective-permute-start | bytes 16908296 | tf_op jit(solution)/shard_map/ppermute | solution.py:128
  97.6 63.7 %collective-permute-start.20 = (bf16[688,2048]{1,0:T(8,128)(2,1)}, bf16[688,2048]{1,0:T(8,128)(2,1)S(1)}, u32[]{:S(2)}, u32[]{:S(2)}) collective-permute-start(bf16[688,2048]{1,0:T(8,128)(2,1)} %collective-permute-done.19), channel_id=1, source_target_pairs={{0,4},{4,0},{1,5},{5,1},{2,6},{6,2},{3,7},{7,3}} | collective-permute-start | bytes 8454152 | tf_op jit(solution)/shard_map/ppermute | solution.py:122
  128.4 85.3 %collective-permute-start.24 = (bf16[1376,2048]{1,0:T(8,128)(2,1)}, bf16[1376,2048]{1,0:T(8,128)(2,1)}, u32[]{:S(2)}, u32[]{:S(2)}) collective-permute-start(bf16[1376,2048]{1,0:T(8,128)(2,1)} %dynamic-slice_bitcast_fusion.4), channel_id=1, source_target_pairs={{0,1},{1,0},{2,3},{3,2},{4,5},{5,4},{6,7},{7,6}} | collective-permute-start | bytes 16908296 | tf_op jit(solution)/shard_map/ppermute | solution.py:128
  137.0 84.9 %collective-permute-start.23 = (bf16[1376,2048]{1,0:T(8,128)(2,1)}, bf16[1376,2048]{1,0:T(8,128)(2,1)}, u32[]{:S(2)}, u32[]{:S(2)}) collective-permute-start(bf16[1376,2048]{1,0:T(8,128)(2,1)} %dynamic-slice_bitcast_fusion.5), channel_id=1, source_target_pairs={{0,1},{1,0},{2,3},{3,2},{4,5},{5,4},{6,7},{7,6}} | collective-permute-start | bytes 16908296 | tf_op jit(solution)/shard_map/ppermute | solution.py:128
  332.9 67.8 %collective-permute-start = (f32[256,2048]{1,0:T(8,128)}, f32[256,2048]{1,0:T(8,128)}, u32[]{:S(2)}, u32[]{:S(2)}) collective-permute-start(f32[256,2048]{1,0:T(8,128)} %get-tuple-element.1451), channel_id=1, source_target_pairs={{0,4},{4,0},{1,5},{5,1},{2,6},{6,2},{3,7},{7,3}} | collective-permute-start | bytes 6291464 | tf_op jit(solution)/shard_map/while/body/ppermute | solution.py:122
  334.4 63.6 %collective-permute-start.1 = (bf16[256,2048]{1,0:T(8,128)(2,1)S(1)}, bf16[256,2048]{1,0:T(8,128)(2,1)}, u32[]{:S(2)}, u32[]{:S(2)}) collective-permute-start(bf16[256,2048]{1,0:T(8,128)(2,1)S(1)} %get-tuple-element.1452), channel_id=1, source_target_pairs={{0,2},{1,3},{2,0},{3,1},{4,6},{5,7},{6,4},{7,5}} | collective-permute-start | bytes 3145736 | tf_op jit(solution)/shard_map/while/body/ppermute | solution.py:125
  416.6 66.7 %collective-permute-start = (f32[256,2048]{1,0:T(8,128)}, f32[256,2048]{1,0:T(8,128)}, u32[]{:S(2)}, u32[]{:S(2)}) collective-permute-start(f32[256,2048]{1,0:T(8,128)} %get-tuple-element.1451), channel_id=1, source_target_pairs={{0,4},{4,0},{1,5},{5,1},{2,6},{6,2},{3,7},{7,3}} | collective-permute-start | bytes 6291464 | tf_op jit(solution)/shard_map/while/body/ppermute | solution.py:122
  418.1 62.4 %collective-permute-start.1 = (bf16[256,2048]{1,0:T(8,128)(2,1)S(1)}, bf16[256,2048]{1,0:T(8,128)(2,1)}, u32[]{:S(2)}, u32[]{:S(2)}) collective-permute-start(bf16[256,2048]{1,0:T(8,128)(2,1)S(1)} %get-tuple-element.1452), channel_id=1, source_target_pairs={{0,2},{1,3},{2,0},{3,1},{4,6},{5,7},{6,4},{7,5}} | collective-permute-start | bytes 3145736 | tf_op jit(solution)/shard_map/while/body/ppermute | solution.py:125
  499.8 65.8 %collective-permute-start = (f32[256,2048]{1,0:T(8,128)}, f32[256,2048]{1,0:T(8,128)}, u32[]{:S(2)}, u32[]{:S(2)}) collective-permute-start(f32[256,2048]{1,0:T(8,128)} %get-tuple-element.1451), channel_id=1, source_target_pairs={{0,4},{4,0},{1,5},{5,1},{2,6},{6,2},{3,7},{7,3}} | collective-permute-start | bytes 6291464 | tf_op jit(solution)/shard_map/while/body/ppermute | solution.py:122
  501.3 61.6 %collective-permute-start.1 = (bf16[256,2048]{1,0:T(8,128)(2,1)S(1)}, bf16[256,2048]{1,0:T(8,128)(2,1)}, u32[]{:S(2)}, u32[]{:S(2)}) collective-permute-start(bf16[256,2048]{1,0:T(8,128)(2,1)S(1)} %get-tuple-element.1452), channel_id=1, source_target_pairs={{0,2},{1,3},{2,0},{3,1},{4,6},{5,7},{6,4},{7,5}} | collective-permute-start | bytes 3145736 | tf_op jit(solution)/shard_map/while/body/ppermute | solution.py:125
  582.1 65.0 %collective-permute-start = (f32[256,2048]{1,0:T(8,128)}, f32[256,2048]{1,0:T(8,128)}, u32[]{:S(2)}, u32[]{:S(2)}) collective-permute-start(f32[256,2048]{1,0:T(8,128)} %get-tuple-element.1451), channel_id=1, source_target_pairs={{0,4},{4,0},{1,5},{5,1},{2,6},{6,2},{3,7},{7,3}} | collective-permute-start | bytes 6291464 | tf_op jit(solution)/shard_map/while/body/ppermute | solution.py:122
  583.6 60.7 %collective-permute-start.1 = (bf16[256,2048]{1,0:T(8,128)(2,1)S(1)}, bf16[256,2048]{1,0:T(8,128)(2,1)}, u32[]{:S(2)}, u32[]{:S(2)}) collective-permute-start(bf16[256,2048]{1,0:T(8,128)(2,1)S(1)} %get-tuple-element.1452), channel_id=1, source_target_pairs={{0,2},{1,3},{2,0},{3,1},{4,6},{5,7},{6,4},{7,5}} | collective-permute-start | bytes 3145736 | tf_op jit(solution)/shard_map/while/body/ppermute | solution.py:125
  663.6 64.1 %collective-permute-start = (f32[256,2048]{1,0:T(8,128)}, f32[256,2048]{1,0:T(8,128)}, u32[]{:S(2)}, u32[]{:S(2)}) collective-permute-start(f32[256,2048]{1,0:T(8,128)} %get-tuple-element.1451), channel_id=1, source_target_pairs={{0,4},{4,0},{1,5},{5,1},{2,6},{6,2},{3,7},{7,3}} | collective-permute-start | bytes 6291464 | tf_op jit(solution)/shard_map/while/body/ppermute | solution.py:122
  665.1 59.9 %collective-permute-start.1 = (bf16[256,2048]{1,0:T(8,128)(2,1)S(1)}, bf16[256,2048]{1,0:T(8,128)(2,1)}, u32[]{:S(2)}, u32[]{:S(2)}) collective-permute-start(bf16[256,2048]{1,0:T(8,128)(2,1)S(1)} %get-tuple-element.1452), channel_id=1, source_target_pairs={{0,2},{1,3},{2,0},{3,1},{4,6},{5,7},{6,4},{7,5}} | collective-permute-start | bytes 3145736 | tf_op jit(solution)/shard_map/while/body/ppermute | solution.py:125
  744.2 63.3 %collective-permute-start = (f32[256,2048]{1,0:T(8,128)}, f32[256,2048]{1,0:T(8,128)}, u32[]{:S(2)}, u32[]{:S(2)}) collective-permute-start(f32[256,2048]{1,0:T(8,128)} %get-tuple-element.1451), channel_id=1, source_target_pairs={{0,4},{4,0},{1,5},{5,1},{2,6},{6,2},{3,7},{7,3}} | collective-permute-start | bytes 6291464 | tf_op jit(solution)/shard_map/while/body/ppermute | solution.py:122
  745.8 59.0 %collective-permute-start.1 = (bf16[256,2048]{1,0:T(8,128)(2,1)S(1)}, bf16[256,2048]{1,0:T(8,128)(2,1)}, u32[]{:S(2)}, u32[]{:S(2)}) collective-permute-start(bf16[256,2048]{1,0:T(8,128)(2,1)S(1)} %get-tuple-element.1452), channel_id=1, source_target_pairs={{0,2},{1,3},{2,0},{3,1},{4,6},{5,7},{6,4},{7,5}} | collective-permute-start | bytes 3145736 | tf_op jit(solution)/shard_map/while/body/ppermute | solution.py:125
  823.9 62.4 %collective-permute-start = (f32[256,2048]{1,0:T(8,128)}, f32[256,2048]{1,0:T(8,128)}, u32[]{:S(2)}, u32[]{:S(2)}) collective-permute-start(f32[256,2048]{1,0:T(8,128)} %get-tuple-element.1451), channel_id=1, source_target_pairs={{0,4},{4,0},{1,5},{5,1},{2,6},{6,2},{3,7},{7,3}} | collective-permute-start | bytes 6291464 | tf_op jit(solution)/shard_map/while/body/ppermute | solution.py:122
  825.4 58.1 %collective-permute-start.1 = (bf16[256,2048]{1,0:T(8,128)(2,1)S(1)}, bf16[256,2048]{1,0:T(8,128)(2,1)}, u32[]{:S(2)}, u32[]{:S(2)}) collective-permute-start(bf16[256,2048]{1,0:T(8,128)(2,1)S(1)} %get-tuple-element.1452), channel_id=1, source_target_pairs={{0,2},{1,3},{2,0},{3,1},{4,6},{5,7},{6,4},{7,5}} | collective-permute-start | bytes 3145736 | tf_op jit(solution)/shard_map/while/body/ppermute | solution.py:125
  902.8 61.6 %collective-permute-start = (f32[256,2048]{1,0:T(8,128)}, f32[256,2048]{1,0:T(8,128)}, u32[]{:S(2)}, u32[]{:S(2)}) collective-permute-start(f32[256,2048]{1,0:T(8,128)} %get-tuple-element.1451), channel_id=1, source_target_pairs={{0,4},{4,0},{1,5},{5,1},{2,6},{6,2},{3,7},{7,3}} | collective-permute-start | bytes 6291464 | tf_op jit(solution)/shard_map/while/body/ppermute | solution.py:122
  904.3 57.3 %collective-permute-start.1 = (bf16[256,2048]{1,0:T(8,128)(2,1)S(1)}, bf16[256,2048]{1,0:T(8,128)(2,1)}, u32[]{:S(2)}, u32[]{:S(2)}) collective-permute-start(bf16[256,2048]{1,0:T(8,128)(2,1)S(1)} %get-tuple-element.1452), channel_id=1, source_target_pairs={{0,2},{1,3},{2,0},{3,1},{4,6},{5,7},{6,4},{7,5}} | collective-permute-start | bytes 3145736 | tf_op jit(solution)/shard_map/while/body/ppermute | solution.py:125
  1205.2 93.0 %collective-permute-start.32 = (bf16[1024,2048]{1,0:T(8,128)(2,1)S(1)}, bf16[1024,2048]{1,0:T(8,128)(2,1)S(1)}, u32[]{:S(2)}, u32[]{:S(2)}) collective-permute-start(bf16[1024,2048]{1,0:T(8,128)(2,1)S(1)} %pad_maximum_fusion.6), channel_id=1, source_target_pairs={{0,2},{1,3},{2,0},{3,1},{4,6},{5,7},{6,4},{7,5}} | collective-permute-start | bytes 12582920 | tf_op jit(solution)/shard_map/ppermute | solution.py:125
  1205.5 93.4 %collective-permute-start.33 = (bf16[1024,2048]{1,0:T(8,128)(2,1)S(1)}, bf16[1024,2048]{1,0:T(8,128)(2,1)S(1)}, u32[]{:S(2)}, u32[]{:S(2)}) collective-permute-start(bf16[1024,2048]{1,0:T(8,128)(2,1)S(1)} %pad_maximum_fusion.6), channel_id=1, source_target_pairs={{0,4},{4,0},{1,5},{5,1},{2,6},{6,2},{3,7},{7,3}} | collective-permute-start | bytes 12582920 | tf_op jit(solution)/shard_map/ppermute | solution.py:122
  1350.7 63.0 %collective-permute-start.36 = (bf16[4096,2048]{1,0:T(8,128)(2,1)}, bf16[4096,2048]{1,0:T(8,128)(2,1)}, u32[]{:S(2)}, u32[]{:S(2)}) collective-permute-start(bf16[4096,2048]{1,0:T(8,128)(2,1)} %get-tuple-element.985), channel_id=1, source_target_pairs={{0,1},{1,0},{2,3},{3,2},{4,5},{5,4},{6,7},{7,6}} | collective-permute-start | bytes 50331656 | tf_op jit(solution)/shard_map/ppermute | solution.py:128
  1488.2 66.6 %collective-permute-start.9 = (f32[256,2048]{1,0:T(8,128)}, f32[256,2048]{1,0:T(8,128)}, u32[]{:S(2)}, u32[]{:S(2)}) collective-permute-start(f32[256,2048]{1,0:T(8,128)} %get-tuple-element.1577), channel_id=1, source_target_pairs={{0,4},{4,0},{1,5},{5,1},{2,6},{6,2},{3,7},{7,3}} | collective-permute-start | bytes 6291464 | tf_op jit(solution)/shard_map/while/body/ppermute | solution.py:122
  1488.7 63.3 %collective-permute-start.10 = (bf16[256,2048]{1,0:T(8,128)(2,1)S(1)}, bf16[256,2048]{1,0:T(8,128)(2,1)}, u32[]{:S(2)}, u32[]{:S(2)}) collective-permute-start(bf16[256,2048]{1,0:T(8,128)(2,1)S(1)} %get-tuple-element.1578), channel_id=1, source_target_pairs={{0,2},{1,3},{2,0},{3,1},{4,6},{5,7},{6,4},{7,5}} | collective-permute-start | bytes 3145736 | tf_op jit(solution)/shard_map/while/body/ppermute | solution.py:125
  1569.9 67.7 %collective-permute-start.9 = (f32[256,2048]{1,0:T(8,128)}, f32[256,2048]{1,0:T(8,128)}, u32[]{:S(2)}, u32[]{:S(2)}) collective-permute-start(f32[256,2048]{1,0:T(8,128)} %get-tuple-element.1577), channel_id=1, source_target_pairs={{0,4},{4,0},{1,5},{5,1},{2,6},{6,2},{3,7},{7,3}} | collective-permute-start | bytes 6291464 | tf_op jit(solution)/shard_map/while/body/ppermute | solution.py:122
  1570.4 64.5 %collective-permute-start.10 = (bf16[256,2048]{1,0:T(8,128)(2,1)S(1)}, bf16[256,2048]{1,0:T(8,128)(2,1)}, u32[]{:S(2)}, u32[]{:S(2)}) collective-permute-start(bf16[256,2048]{1,0:T(8,128)(2,1)S(1)} %get-tuple-element.1578), channel_id=1, source_target_pairs={{0,2},{1,3},{2,0},{3,1},{4,6},{5,7},{6,4},{7,5}} | collective-permute-start | bytes 3145736 | tf_op jit(solution)/shard_map/while/body/ppermute | solution.py:125
  1652.7 68.9 %collective-permute-start.9 = (f32[256,2048]{1,0:T(8,128)}, f32[256,2048]{1,0:T(8,128)}, u32[]{:S(2)}, u32[]{:S(2)}) collective-permute-start(f32[256,2048]{1,0:T(8,128)} %get-tuple-element.1577), channel_id=1, source_target_pairs={{0,4},{4,0},{1,5},{5,1},{2,6},{6,2},{3,7},{7,3}} | collective-permute-start | bytes 6291464 | tf_op jit(solution)/shard_map/while/body/ppermute | solution.py:122
  1653.2 65.6 %collective-permute-start.10 = (bf16[256,2048]{1,0:T(8,128)(2,1)S(1)}, bf16[256,2048]{1,0:T(8,128)(2,1)}, u32[]{:S(2)}, u32[]{:S(2)}) collective-permute-start(bf16[256,2048]{1,0:T(8,128)(2,1)S(1)} %get-tuple-element.1578), channel_id=1, source_target_pairs={{0,2},{1,3},{2,0},{3,1},{4,6},{5,7},{6,4},{7,5}} | collective-permute-start | bytes 3145736 | tf_op jit(solution)/shard_map/while/body/ppermute | solution.py:125
  1736.6 68.1 %collective-permute-start.9 = (f32[256,2048]{1,0:T(8,128)}, f32[256,2048]{1,0:T(8,128)}, u32[]{:S(2)}, u32[]{:S(2)}) collective-permute-start(f32[256,2048]{1,0:T(8,128)} %get-tuple-element.1577), channel_id=1, source_target_pairs={{0,4},{4,0},{1,5},{5,1},{2,6},{6,2},{3,7},{7,3}} | collective-permute-start | bytes 6291464 | tf_op jit(solution)/shard_map/while/body/ppermute | solution.py:122
  1737.1 64.9 %collective-permute-start.10 = (bf16[256,2048]{1,0:T(8,128)(2,1)S(1)}, bf16[256,2048]{1,0:T(8,128)(2,1)}, u32[]{:S(2)}, u32[]{:S(2)}) collective-permute-start(bf16[256,2048]{1,0:T(8,128)(2,1)S(1)} %get-tuple-element.1578), channel_id=1, source_target_pairs={{0,2},{1,3},{2,0},{3,1},{4,6},{5,7},{6,4},{7,5}} | collective-permute-start | bytes 3145736 | tf_op jit(solution)/shard_map/while/body/ppermute | solution.py:125
  1819.8 67.3 %collective-permute-start.9 = (f32[256,2048]{1,0:T(8,128)}, f32[256,2048]{1,0:T(8,128)}, u32[]{:S(2)}, u32[]{:S(2)}) collective-permute-start(f32[256,2048]{1,0:T(8,128)} %get-tuple-element.1577), channel_id=1, source_target_pairs={{0,4},{4,0},{1,5},{5,1},{2,6},{6,2},{3,7},{7,3}} | collective-permute-start | bytes 6291464 | tf_op jit(solution)/shard_map/while/body/ppermute | solution.py:122
  1820.3 64.0 %collective-permute-start.10 = (bf16[256,2048]{1,0:T(8,128)(2,1)S(1)}, bf16[256,2048]{1,0:T(8,128)(2,1)}, u32[]{:S(2)}, u32[]{:S(2)}) collective-permute-start(bf16[256,2048]{1,0:T(8,128)(2,1)S(1)} %get-tuple-element.1578), channel_id=1, source_target_pairs={{0,2},{1,3},{2,0},{3,1},{4,6},{5,7},{6,4},{7,5}} | collective-permute-start | bytes 3145736 | tf_op jit(solution)/shard_map/while/body/ppermute | solution.py:125
  1902.3 66.4 %collective-permute-start.9 = (f32[256,2048]{1,0:T(8,128)}, f32[256,2048]{1,0:T(8,128)}, u32[]{:S(2)}, u32[]{:S(2)}) collective-permute-start(f32[256,2048]{1,0:T(8,128)} %get-tuple-element.1577), channel_id=1, source_target_pairs={{0,4},{4,0},{1,5},{5,1},{2,6},{6,2},{3,7},{7,3}} | collective-permute-start | bytes 6291464 | tf_op jit(solution)/shard_map/while/body/ppermute | solution.py:122
  1902.8 63.2 %collective-permute-start.10 = (bf16[256,2048]{1,0:T(8,128)(2,1)S(1)}, bf16[256,2048]{1,0:T(8,128)(2,1)}, u32[]{:S(2)}, u32[]{:S(2)}) collective-permute-start(bf16[256,2048]{1,0:T(8,128)(2,1)S(1)} %get-tuple-element.1578), channel_id=1, source_target_pairs={{0,2},{1,3},{2,0},{3,1},{4,6},{5,7},{6,4},{7,5}} | collective-permute-start | bytes 3145736 | tf_op jit(solution)/shard_map/while/body/ppermute | solution.py:125
  1983.7 65.5 %collective-permute-start.9 = (f32[256,2048]{1,0:T(8,128)}, f32[256,2048]{1,0:T(8,128)}, u32[]{:S(2)}, u32[]{:S(2)}) collective-permute-start(f32[256,2048]{1,0:T(8,128)} %get-tuple-element.1577), channel_id=1, source_target_pairs={{0,4},{4,0},{1,5},{5,1},{2,6},{6,2},{3,7},{7,3}} | collective-permute-start | bytes 6291464 | tf_op jit(solution)/shard_map/while/body/ppermute | solution.py:122
  1984.2 62.3 %collective-permute-start.10 = (bf16[256,2048]{1,0:T(8,128)(2,1)S(1)}, bf16[256,2048]{1,0:T(8,128)(2,1)}, u32[]{:S(2)}, u32[]{:S(2)}) collective-permute-start(bf16[256,2048]{1,0:T(8,128)(2,1)S(1)} %get-tuple-element.1578), channel_id=1, source_target_pairs={{0,2},{1,3},{2,0},{3,1},{4,6},{5,7},{6,4},{7,5}} | collective-permute-start | bytes 3145736 | tf_op jit(solution)/shard_map/while/body/ppermute | solution.py:125
  2064.4 64.7 %collective-permute-start.9 = (f32[256,2048]{1,0:T(8,128)}, f32[256,2048]{1,0:T(8,128)}, u32[]{:S(2)}, u32[]{:S(2)}) collective-permute-start(f32[256,2048]{1,0:T(8,128)} %get-tuple-element.1577), channel_id=1, source_target_pairs={{0,4},{4,0},{1,5},{5,1},{2,6},{6,2},{3,7},{7,3}} | collective-permute-start | bytes 6291464 | tf_op jit(solution)/shard_map/while/body/ppermute | solution.py:122
  2064.9 61.4 %collective-permute-start.10 = (bf16[256,2048]{1,0:T(8,128)(2,1)S(1)}, bf16[256,2048]{1,0:T(8,128)(2,1)}, u32[]{:S(2)}, u32[]{:S(2)}) collective-permute-start(bf16[256,2048]{1,0:T(8,128)(2,1)S(1)} %get-tuple-element.1578), channel_id=1, source_target_pairs={{0,2},{1,3},{2,0},{3,1},{4,6},{5,7},{6,4},{7,5}} | collective-permute-start | bytes 3145736 | tf_op jit(solution)/shard_map/while/body/ppermute | solution.py:125
  2135.8 132.5 %collective-permute-start.46 = (bf16[1376,2048]{1,0:T(8,128)(2,1)}, bf16[1376,2048]{1,0:T(8,128)(2,1)}, u32[]{:S(2)}, u32[]{:S(2)}) collective-permute-start(bf16[1376,2048]{1,0:T(8,128)(2,1)} %get-tuple-element.972), channel_id=1, source_target_pairs={{0,1},{1,0},{2,3},{3,2},{4,5},{5,4},{6,7},{7,6}} | collective-permute-start | bytes 16908296 | tf_op jit(solution)/shard_map/ppermute | solution.py:128
  2146.3 134.3 %collective-permute-start.47 = (bf16[1376,2048]{1,0:T(8,128)(2,1)}, bf16[1376,2048]{1,0:T(8,128)(2,1)}, u32[]{:S(2)}, u32[]{:S(2)}) collective-permute-start(bf16[1376,2048]{1,0:T(8,128)(2,1)} %get-tuple-element.970), channel_id=1, source_target_pairs={{0,1},{1,0},{2,3},{3,2},{4,5},{5,4},{6,7},{7,6}} | collective-permute-start | bytes 16908296 | tf_op jit(solution)/shard_map/ppermute | solution.py:128
  2315.7 90.1 %collective-permute-start.52 = (bf16[1376,2048]{1,0:T(8,128)(2,1)}, bf16[1376,2048]{1,0:T(8,128)(2,1)}, u32[]{:S(2)}, u32[]{:S(2)}) collective-permute-start(bf16[1376,2048]{1,0:T(8,128)(2,1)} %get-tuple-element.962), channel_id=1, source_target_pairs={{0,1},{1,0},{2,3},{3,2},{4,5},{5,4},{6,7},{7,6}} | collective-permute-start | bytes 16908296 | tf_op jit(solution)/shard_map/ppermute | solution.py:128
  2329.2 88.8 %collective-permute-start.51 = (bf16[1376,2048]{1,0:T(8,128)(2,1)}, bf16[1376,2048]{1,0:T(8,128)(2,1)}, u32[]{:S(2)}, u32[]{:S(2)}) collective-permute-start(bf16[1376,2048]{1,0:T(8,128)(2,1)} %get-tuple-element.964), channel_id=1, source_target_pairs={{0,1},{1,0},{2,3},{3,2},{4,5},{5,4},{6,7},{7,6}} | collective-permute-start | bytes 16908296 | tf_op jit(solution)/shard_map/ppermute | solution.py:128
  2357.6 72.5 %collective-permute-start.50 = (bf16[1376,2048]{1,0:T(8,128)(2,1)}, bf16[1376,2048]{1,0:T(8,128)(2,1)}, u32[]{:S(2)}, u32[]{:S(2)}) collective-permute-start(bf16[1376,2048]{1,0:T(8,128)(2,1)} %get-tuple-element.966), channel_id=1, source_target_pairs={{0,1},{1,0},{2,3},{3,2},{4,5},{5,4},{6,7},{7,6}} | collective-permute-start | bytes 16908296 | tf_op jit(solution)/shard_map/ppermute | solution.py:128
  2402.9 92.8 %collective-permute-start.49 = (bf16[1024,2048]{1,0:T(8,128)(2,1)}, bf16[1024,2048]{1,0:T(8,128)(2,1)}, u32[]{:S(2)}, u32[]{:S(2)}) collective-permute-start(bf16[1024,2048]{1,0:T(8,128)(2,1)} %pad_maximum_fusion.7), channel_id=1, source_target_pairs={{0,4},{4,0},{1,5},{5,1},{2,6},{6,2},{3,7},{7,3}} | collective-permute-start | bytes 12582920 | tf_op jit(solution)/shard_map/ppermute | solution.py:122
  (185 other events, 6101.9 us)
